TPU v7x, 128 devices: a whole 4x4x4 slice. The times are simulated.
128 devices in a mesh: dp: 1, tp: 64 (over z, y, x), cp: 2 (over core).
Axes of the slice: x: 4, y: 4, z: 4, core: 2. Of those that a mesh axis runs over, the one named last changes fastest.
Arguments:
- c_latent: bfloat16 [4096, 512], P(('dp', 'cp'))
- k_rope: bfloat16 [4096, 64], P(('dp', 'cp'))
- q_heads: bfloat16 [4096, 128, 192], P(('dp', 'cp'), 'tp')
- d_out: bfloat16 [4096, 128, 128], P(('dp', 'cp'), 'tp')
- w_uk: bfloat16 [512, 128, 128], P(None, 'tp')
- w_uv: bfloat16 [512, 128, 128], P(None, 'tp')
Outputs:
- output 1: bfloat16 [4096, 128, 128], P(('dp', 'cp'), 'tp')
- output 2: float32 [4096, 128, 192], P(('dp', 'cp'), 'tp')
- output 3: float32 [4096, 512], P(('dp', 'cp'))
- output 4: float32 [4096, 64], P(('dp', 'cp'))
- output 5: float32 [512, 128, 128], P('dp', 'tp')
- output 6: float32 [512, 128, 128], P('dp', 'tp')
All inputs are finite; a program needn't handle non-finite values.
Results may differ from a plain program's by a relative error of at most 0.0114719.
Values are sent between devices in bfloat16 or wider.
A program may use at most 1 GiB of HBM per device.

v0:
```python
import jax
import jax.numpy as jnp
from jax import lax
from jax.sharding import PartitionSpec as P

NEG_BIG = -1.0e30


def project_block(c_blk, w_uk, w_uv):
    knope_blk = jnp.einsum('kr,rhd->khd', c_blk, w_uk, preferred_element_type=jnp.float32)
    v_blk = jnp.einsum('kr,rhd->khd', c_blk, w_uv, preferred_element_type=jnp.float32)
    return knope_blk.astype(jnp.bfloat16), v_blk.astype(jnp.bfloat16)


def block_scores(q_nope, q_rope, knope_blk, rope_blk, qk_scale, key_mask):
    scores = jnp.einsum('qhd,khd->qhk', q_nope, knope_blk, preferred_element_type=jnp.float32)
    scores = scores + jnp.einsum('qhd,kd->qhk', q_rope, rope_blk, preferred_element_type=jnp.float32)
    scores = scores * qk_scale
    if key_mask is None:
        return scores
    return jnp.where(key_mask[:, None, :], scores, NEG_BIG)


def forward_update(soft_state, q_nope, q_rope, c_blk, rope_blk, w_uk, w_uv, qk_scale, key_mask):
    run_max, run_sum, out_acc = soft_state
    knope_blk, v_blk = project_block(c_blk, w_uk, w_uv)
    scores = block_scores(q_nope, q_rope, knope_blk, rope_blk, qk_scale, key_mask)
    new_max = jnp.maximum(run_max, jnp.max(scores, axis=-1))
    rescale = jnp.exp(run_max - new_max)
    prob_blk = jnp.exp(scores - new_max[..., None])
    new_sum = run_sum * rescale + jnp.sum(prob_blk, axis=-1)
    pv_part = jnp.einsum('qhk,khd->qhd', prob_blk.astype(jnp.bfloat16), v_blk, preferred_element_type=jnp.float32)
    return (new_max, new_sum, out_acc * rescale[..., None] + pv_part)


def backward_block(q_nope, q_rope, d_out, log_norm, d_dot, c_blk, rope_blk, w_uk, w_uv, qk_scale, key_mask):
    knope_blk, v_blk = project_block(c_blk, w_uk, w_uv)
    scores = block_scores(q_nope, q_rope, knope_blk, rope_blk, qk_scale, key_mask)
    prob_blk = jnp.exp(scores - log_norm[..., None])
    d_prob = jnp.einsum('qhd,khd->qhk', d_out, v_blk, preferred_element_type=jnp.float32)
    d_score = (prob_blk * (d_prob - d_dot[..., None]) * qk_scale).astype(jnp.bfloat16)
    dq_nope = jnp.einsum('qhk,khd->qhd', d_score, knope_blk, preferred_element_type=jnp.float32)
    dq_rope = jnp.einsum('qhk,kd->qhd', d_score, rope_blk, preferred_element_type=jnp.float32)
    dk_nope = jnp.einsum('qhk,qhd->khd', d_score, q_nope, preferred_element_type=jnp.float32).astype(jnp.bfloat16)
    dk_rope = jnp.einsum('qhk,qhd->kd', d_score, q_rope, preferred_element_type=jnp.float32)
    dv_blk = jnp.einsum('qhk,qhd->khd', prob_blk.astype(jnp.bfloat16), d_out, preferred_element_type=jnp.float32).astype(jnp.bfloat16)
    dc_blk = jnp.einsum('khd,rhd->kr', dk_nope, w_uk, preferred_element_type=jnp.float32) + jnp.einsum('khd,rhd->kr', dv_blk, w_uv, preferred_element_type=jnp.float32)
    dw_k = jnp.einsum('kr,khd->rhd', c_blk, dk_nope, preferred_element_type=jnp.float32)
    dw_v = jnp.einsum('kr,khd->rhd', c_blk, dv_blk, preferred_element_type=jnp.float32)
    return (dq_nope, dq_rope, dc_blk, dk_rope, dw_k, dw_v)


def add_lower(full_arr, part_arr):
    split_at = part_arr.shape[0]
    return jnp.concatenate([full_arr[:split_at] + part_arr, full_arr[split_at:]], axis=0)


def add_upper(full_arr, part_arr):
    split_at = full_arr.shape[0] - part_arr.shape[0]
    return jnp.concatenate([full_arr[:split_at], full_arr[split_at:] + part_arr], axis=0)


def solution(mesh):
    n_cp = mesh.shape['cp']
    shift_perm = [(src_dev, (src_dev + 1) % n_cp) for src_dev in range(n_cp)]
    seq_spec = P(('dp', 'cp'), None)
    head_spec = P(('dp', 'cp'), 'tp', None)
    weight_spec = P(None, 'tp', None)
    grad_spec = P('dp', 'tp', None)

    def device_fn(c_latent, k_rope, q_heads, d_out, w_uk, w_uv):
        tok_rows = c_latent.shape[0]
        half_len = tok_rows // 2
        n_heads = q_heads.shape[1]
        d_nope = w_uk.shape[2]
        d_val = w_uv.shape[2]
        qk_scale = q_heads.shape[2] ** -0.5
        my_idx = lax.axis_index('cp')
        q_nope = q_heads[:, :, :d_nope]
        q_rope = q_heads[:, :, d_nope:]
        half_offsets = jnp.arange(half_len)
        positions = jnp.concatenate([my_idx * half_len + half_offsets, (2 * n_cp - 1 - my_idx) * half_len + half_offsets])
        diag_mask = positions[None, :] <= positions[:, None]

        soft_state = (jnp.full((tok_rows, n_heads), NEG_BIG, jnp.float32), jnp.zeros((tok_rows, n_heads), jnp.float32), jnp.zeros((tok_rows, n_heads, d_val), jnp.float32))
        soft_state = forward_update(soft_state, q_nope, q_rope, c_latent, k_rope, w_uk, w_uv, qk_scale, diag_mask)

        def forward_hop(hop_idx, loop_carry):
            c_blk, rope_blk, state_in = loop_carry
            c_blk = lax.ppermute(c_blk, 'cp', shift_perm)
            rope_blk = lax.ppermute(rope_blk, 'cp', shift_perm)
            src_idx = (my_idx - hop_idx) % n_cp

            def earlier_keys(state_cur):
                return forward_update(state_cur, q_nope, q_rope, c_blk[:half_len], rope_blk[:half_len], w_uk, w_uv, qk_scale, None)

            def later_queries(state_cur):
                upper_state = forward_update(tuple(part_arr[half_len:] for part_arr in state_cur), q_nope[half_len:], q_rope[half_len:], c_blk, rope_blk, w_uk, w_uv, qk_scale, None)
                return tuple(jnp.concatenate([old_arr[:half_len], new_arr], axis=0) for old_arr, new_arr in zip(state_cur, upper_state))

            return (c_blk, rope_blk, lax.cond(src_idx < my_idx, earlier_keys, later_queries, state_in))

        soft_state = lax.fori_loop(1, n_cp, forward_hop, (c_latent, k_rope, soft_state))[2]
        run_max, run_sum, out_acc = soft_state
        out_wide = out_acc / run_sum[..., None]
        log_norm = run_max + jnp.log(run_sum)
        d_dot = jnp.sum(d_out.astype(jnp.float32) * out_wide, axis=-1)
        grad_acc = backward_block(q_nope, q_rope, d_out, log_norm, d_dot, c_latent, k_rope, w_uk, w_uv, qk_scale, diag_mask)

        def backward_hop(hop_idx, loop_carry):
            c_blk, rope_blk, acc_in = loop_carry
            c_blk = lax.ppermute(c_blk, 'cp', shift_perm)
            rope_blk = lax.ppermute(rope_blk, 'cp', shift_perm)
            dc_acc = lax.ppermute(acc_in[2], 'cp', shift_perm)
            drope_acc = lax.ppermute(acc_in[3], 'cp', shift_perm)
            src_idx = (my_idx - hop_idx) % n_cp

            def earlier_keys(acc_cur):
                blk_grads = backward_block(q_nope, q_rope, d_out, log_norm, d_dot, c_blk[:half_len], rope_blk[:half_len], w_uk, w_uv, qk_scale, None)
                return (acc_cur[0] + blk_grads[0], acc_cur[1] + blk_grads[1], add_lower(acc_cur[2], blk_grads[2]), add_lower(acc_cur[3], blk_grads[3]), acc_cur[4] + blk_grads[4], acc_cur[5] + blk_grads[5])

            def later_queries(acc_cur):
                blk_grads = backward_block(q_nope[half_len:], q_rope[half_len:], d_out[half_len:], log_norm[half_len:], d_dot[half_len:], c_blk, rope_blk, w_uk, w_uv, qk_scale, None)
                return (add_upper(acc_cur[0], blk_grads[0]), add_upper(acc_cur[1], blk_grads[1]), acc_cur[2] + blk_grads[2], acc_cur[3] + blk_grads[3], acc_cur[4] + blk_grads[4], acc_cur[5] + blk_grads[5])

            acc_mid = (acc_in[0], acc_in[1], dc_acc, drope_acc, acc_in[4], acc_in[5])
            return (c_blk, rope_blk, lax.cond(src_idx < my_idx, earlier_keys, later_queries, acc_mid))

        grad_acc = lax.fori_loop(1, n_cp, backward_hop, (c_latent, k_rope, grad_acc))[2]
        dq_nope, dq_rope, dc_acc, drope_acc, dw_k, dw_v = grad_acc
        dc_acc = lax.ppermute(dc_acc, 'cp', shift_perm)
        drope_acc = lax.ppermute(drope_acc, 'cp', shift_perm)
        return (out_wide.astype(jnp.bfloat16),
                jnp.concatenate([dq_nope, dq_rope], axis=-1),
                lax.psum(dc_acc, 'tp'),
                lax.psum(drope_acc, 'tp'),
                lax.psum(dw_k, 'cp'),
                lax.psum(dw_v, 'cp'))

    return jax.shard_map(device_fn, mesh=mesh,
                         in_specs=(seq_spec, seq_spec, head_spec, head_spec, weight_spec, weight_spec),
                         out_specs=(head_spec, head_spec, seq_spec, seq_spec, grad_spec, grad_spec),
                         check_vma=False)
```

profile of v0, /device:TPU:1, one launch (start us, length us, event | category | flops | bytes accessed | tf_op | source)
XLA Modules:
  0.0 506.6 jit_solution(153208936846051031)
XLA Ops:
  7.2 1.4 collective-permute-start.1
  8.8 2.3 convolution_convert_fusion.11
  11.1 2.7 convolution_convert_fusion.12
  13.8 2.9 broadcast_compare_fusion
  16.8 13.1 %fusion.193 = f32[2,2048,2048]{2,1,0:T(8,128)} fusion(bf16[2048,2,128]{2,0,1:T(8,128)(2,1)S(1)} %convolution_convert_fusion.12, bf16[2048,2,192]{0,2,1:T(8,128)(2,1)S(1)} %copy-done.21), kind=kOutput, calls=%fused_computation.199 | convolution fusion | flops 2147483648 | bytes 35651584 | tf_op jit(solution)/shard_map/qhd,khd->qhk/dot_general | solution.py:16
  29.9 22.4 %fusion.197 = (f32[2048,2]{0,1:T(2,128)S(1)}, f32[2048,2,2048]{0,2,1:T(8,128)}) fusion(bf16[2048,64]{0,1:T(8,128)(2,1)S(1)} %copy-done.36, bf16[2048,2,192]{0,2,1:T(8,128)(2,1)S(1)} %copy-done.21, f32[2,2048,2048]{2,1,0:T(8,128)} %fusion.193, pred[2048,2048]{0,1:T(8,128)(4,1)S(1)} %broadcast_compare_fusion), kind=kOutput, calls=%fused_computation.203 | convolution fusion | flops 1107292160 | bytes 72105984 | tf_op jit(solution)/shard_map/qhd,kd->qhk/dot_general | solution.py:17
  52.3 13.0 %fusion.146 = f32[2048,2]{0,1:T(2,128)S(1)} fusion(f32[2048,2,2048]{0,2,1:T(8,128)} %get-tuple-element.395, f32[2048,2]{0,1:T(2,128)S(1)} %broadcast_maximum_fusion), kind=kLoop, calls=%fused_computation.151 | loop fusion | flops 16773120 | bytes 33587200 | tf_op jit(solution)/shard_map/reduce_sum | solution.py:31
  65.4 13.6 %fusion.164 = f32[2048,2,128]{0,2,1:T(8,128)S(1)} fusion(bf16[2048,2,128]{2,0,1:T(8,128)(2,1)S(1)} %convolution_convert_fusion.11, f32[2048,2,2048]{0,2,1:T(8,128)} %get-tuple-element.395, f32[2048,2]{0,1:T(2,128)S(1)} %broadcast_maximum_fusion, f32[2048,2]{0,1:T(2,128)S(1)} %get-tuple-element.392), kind=kOutput, calls=%fused_computation.168 | convolution fusion | flops 2164785152 | bytes 36732928 | tf_op jit(solution)/shard_map/qhk,khd->qhd/dot_general | solution.py:32
  79.0 1.9 slice.82
  80.9 1.3 copy.140
  82.3 54.3 %conditional.2 = (f32[2048,2]{0,1:T(2,128)S(1)}, f32[2048,2]{0,1:T(2,128)S(1)}, f32[2048,2,128]{2,1,0:T(2,128)S(1)}) conditional(s32[]{:T(128)} %convert_element_type.107, (f32[2048,2]{0,1:T(2,128)S(1)}, bf16[2048,512]{1,0:T(8,128)(2,1)}, bf16[512,2,128]{2,1,0:T(2,128)(2,1)}, bf16[2048,2,128]{2,0,1:T(8,128)(2,1)}, ...), branch_computations={%region_2.5_spmd.clone, %region_5.8_spmd.clone} | conditional | flops 3789570048 | bytes 102449176 | solution.py:101
  90.2 10.4 %fusion.125 = f32[2,1024,2048]{2,1,0:T(8,128)} fusion(bf16[2048,2,128]{2,0,1:T(8,128)(2,1)} %get-tuple-element.295, bf16[2048,512]{1,0:T(8,128)(2,1)} %get-tuple-element.293, bf16[512,2,128]{2,1,0:T(2,128)(2,1)} %get-tuple-element.294), kind=kOutput, calls=%fused_computation.129 | convolution fusion | flops 1342439424 | bytes 19136512 | tf_op jit(solution)/shard_map/while/body/eval_jaxpr/cond/branch_1_fun/qhd,khd->qhk/dot_general | solution.py:16
  100.6 14.2 %fusion.196 = (f32[2048,2]{0,1:T(2,128)S(1)}, f32[2048,2,1024]{0,2,1:T(8,128)}) fusion(bf16[2048,2,64]{0,2,1:T(8,128)(2,1)} %get-tuple-element.296, bf16[2048,64]{0,1:T(8,128)(2,1)} %get-tuple-element.297, f32[2,1024,2048]{2,1,0:T(8,128)} %fusion.125), kind=kOutput, calls=%fused_computation.202 | convolution fusion | flops 549449728 | bytes 34226176 | tf_op jit(solution)/shard_map/while/body/eval_jaxpr/cond/branch_1_fun/qhd,kd->qhk/dot_general | solution.py:17
  114.9 8.0 %fusion.115 = f32[2048,2]{0,1:T(2,128)S(1)} fusion(f32[2048,2,1024]{0,2,1:T(8,128)} %get-tuple-element.391, f32[2048,2]{0,1:T(2,128)S(1)} %max.7), kind=kLoop, calls=%fused_computation.122 | loop fusion | flops 8384512 | bytes 16809984 | tf_op jit(solution)/shard_map/while/body/eval_jaxpr/cond/branch_1_fun/reduce_sum | solution.py:31
  122.9 10.6 %fusion.122 = f32[2048,2,128]{0,2,1:T(8,128)} fusion(f32[2048,2,1024]{0,2,1:T(8,128)} %get-tuple-element.391, f32[2048,2]{0,1:T(2,128)S(1)} %max.7, f32[2048,2,128]{0,2,1:T(8,128)S(1)} %get-tuple-element.299, f32[2048,2]{0,1:T(2,128)S(1)} %get-tuple-element.383, bf16[2048,512]{1,0:T(8,128)(2,1)} %get-tuple-element.293, ...), kind=kOutput, calls=%fused_computation.126 | convolution fusion | flops 1351876608 | bytes 22315008 | tf_op jit(solution)/shard_map/while/body/eval_jaxpr/cond/branch_1_fun/qhk,khd->qhd/dot_general | solution.py:32
  133.5 2.8 copy.137
  136.6 1.6 copy.80
  138.3 14.3 %fusion.160 = bf16[2048,2,128]{2,0,1:T(8,128)(2,1)} fusion(f32[2048,2,2048]{0,2,1:T(8,128)} %get-tuple-element.395, f32[2048,2]{0,1:T(2,128)S(1)} %get-tuple-element.279, bf16[2048,2,128]{2,1,0:T(2,128)(2,1)S(1)} %copy-done.3), kind=kOutput, calls=%fused_computation.166 | convolution fusion | flops 2164785152 | bytes 35667968 | tf_op jit(solution)/shard_map/qhk,qhd->khd/dot_general | solution.py:46
  152.5 29.5 %multiply_reduce_fusion = (f32[2048,2]{1,0:T(8,128)S(1)}, bf16[2048,2,128]{2,1,0:T(2,128)(2,1)}) fusion(bf16[2048,2,128]{2,1,0:T(2,128)(2,1)S(1)} %copy-done.3, f32[2048,2,128]{2,1,0:T(2,128)S(1)} %copy-done.26, f32[2048,2]{1,0:T(8,128)S(1)} %copy-done.34), kind=kLoop, calls=%fused_computation.176 | loop fusion | flops 2617344 | bytes 4227072 | tf_op jit(solution)/shard_map/reduce_sum | solution.py:107
  182.4 0.6 copy-done.13
  183.0 18.6 %fusion.142 = bf16[2048,2,2048]{0,2,1:T(8,128)(2,1)} fusion(f32[2048,2,2048]{0,2,1:T(8,128)} %get-tuple-element.395, f32[2048,2]{0,1:T(2,128)S(1)} %copy.83, f32[2048,2]{0,1:T(2,128)S(1)} %get-tuple-element.279, bf16[2048,2,128]{2,0,1:T(8,128)(2,1)S(1)} %copy-done.24, bf16[2048,2,128]{2,1,0:T(2,128)(2,1)S(1)} %copy-done.3), kind=kOutput, calls=%fused_computation.144 | convolution fusion | flops 2189426688 | bytes 52461568 | tf_op jit(solution)/shard_map/qhd,khd->qhk/dot_general | solution.py:40
  201.6 11.7 %fusion.163 = bf16[2048,2,128]{2,0,1:T(8,128)(2,1)} fusion(bf16[2048,2,2048]{0,2,1:T(8,128)(2,1)} %fusion.142, bf16[2048,2,192]{0,2,1:T(8,128)(2,1)} %param.12), kind=kOutput, calls=%fused_computation.167 | convolution fusion | flops 2148007936 | bytes 18874368 | tf_op jit(solution)/shard_map/qhk,qhd->khd/dot_general | solution.py:44
  213.3 2.2 fusion.186
  215.4 0.8 bitcast_add_fusion.7
  216.2 3.7 collective-permute-start.2
  220.0 5.2 %convolution_bitcast_fusion.7 = f32[2048,64]{0,1:T(8,128)S(1)} fusion(bf16[2048,2,2048]{0,2,1:T(8,128)(2,1)S(1)} %bitcast.246, bf16[2048,2,192]{0,2,1:T(8,128)(2,1)S(1)} %copy-done.22), kind=kOutput, calls=%fused_computation.169 | convolution fusion | flops 1073741824 | bytes 17825792 | tf_op jit(solution)/shard_map/qhk,qhd->kd/dot_general | solution.py:45
  225.2 0.6 collective-permute-start.3
  225.8 4.0 fusion.181
  229.8 3.8 convolution_bitcast_fusion.6
  233.7 1.5 fusion.176
  235.2 1.5 fusion.173
  236.7 71.8 %conditional.3 = (f32[2048,2,128]{0,2,1:T(8,128)}, f32[2048,2,64]{0,2,1:T(8,128)}, f32[2048,512]{1,0:T(8,128)}, f32[2048,64]{0,1:T(8,128)S(1)}, f32[512,2,128]{0...) conditional(s32[]{:T(128)} %convert_element_type.107, ...), branch_computations={%region_9.10_spmd, %region_10.11_spmd} | conditional | flops 10239606784 | bytes 243425696 | solution.py:127
  243.1 1.6 copy.102
  244.7 1.7 slice.78
  246.4 1.7 convolution_convert_fusion.5
  248.1 3.3 slice.76
  251.3 3.6 fusion.198
  255.0 8.7 %fusion.52 = f32[2048,2,1024]{0,2,1:T(8,128)} fusion(f32[2,1024,2048]{2,1,0:T(8,128)S(1)} %fusion.198, f32[2048,2]{0,1:T(2,128)S(1)} %get-tuple-element.241, bf16[2048,2,64]{0,2,1:T(8,128)(2,1)S(1)} %copy-done.16, bf16[2048,64]{0,1:T(8,128)(2,1)} %get-tuple-element.240), kind=kOutput, calls=%fused_computation.54 | convolution fusion | flops 549453824 | bytes 34226176 | tf_op jit(solution)/shard_map/while/body/eval_jaxpr/cond/branch_1_fun/qhd,kd->qhk/dot_general | solution.py:17
  263.7 8.9 %fusion.60 = bf16[1024,2,128]{2,0,1:T(8,128)(2,1)} fusion(f32[2048,2,1024]{0,2,1:T(8,128)} %fusion.52, bf16[2048,2,128]{2,1,0:T(2,128)(2,1)S(1)} %get-tuple-element.356), kind=kOutput, calls=%fused_computation.67 | convolution fusion | flops 1078198272 | bytes 18350080 | tf_op jit(solution)/shard_map/while/body/eval_jaxpr/cond/branch_1_fun/qhk,qhd->khd/dot_general | solution.py:46
  272.6 10.3 %fusion.49 = bf16[2048,2,1024]{0,2,1:T(8,128)(2,1)} fusion(f32[2048,2,1024]{0,2,1:T(8,128)} %fusion.52, f32[2048,2]{0,1:T(2,128)S(1)} %copy.102, bf16[2048,2,128]{2,1,0:T(2,128)(2,1)S(1)} %get-tuple-element.356, bf16[2048,512]{1,0:T(8,128)(2,1)} %get-tuple-element.236, bf16[512,2,128]{2,1,0:T(2,128)(2,1)S(1)} %get-tuple-element.355), kind=kOutput, calls=%fused_computation.50 | convolution fusion | flops 1359216640 | bytes 27541504 | tf_op jit(solution)/shard_map/while/body/eval_jaxpr/cond/branch_1_fun/qhd,khd->qhk/dot_general | solution.py:40
  283.0 6.3 %fusion.64 = f32[1024,64]{0,1:T(8,128)S(1)} fusion(bf16[2048,2,1024]{0,2,1:T(8,128)(2,1)} %fusion.49, bf16[2048,2,64]{0,2,1:T(8,128)(2,1)} %get-tuple-element.239, f32[2048,64]{0,1:T(8,128)} %get-tuple-element.247), kind=kOutput, calls=%fused_computation.72 | convolution fusion | flops 536936448 | bytes 9437184 | tf_op jit(solution)/shard_map/while/body/eval_jaxpr/cond/branch_1_fun/qhk,qhd->kd/dot_general | solution.py:45
  289.3 2.3 fusion.63
  291.7 2.7 fusion.55
  294.4 3.6 convolution_add_fusion.1
  298.0 2.7 convolution_bitcast_fusion.4
  300.7 2.5 convolution_bitcast_fusion.3
  303.7 2.1 fusion.56
  305.8 2.5 pad_maximum_fusion.2
  308.5 6.4 %collective-permute-start.4 = (f32[2048,512]{1,0:T(8,128)}, f32[2048,512]{1,0:T(8,128)}, u32[]{:S(2)}, u32[]{:S(2)}) collective-permute-start(f32[2048,512]{1,0:T(8,128)} %get-tuple-element.367), channel_id=1, source_target_pairs={{0,1},{1,0},{2,3},{3,2},{4,5},{5,4},{6,7},{7,6},{8,9},{9,8},{10,11... | collective-permute-start | bytes 12582920 | tf_op jit(solution)/shard_map/ppermute | solution.py:131
  315.0 7.4 %collective-permute-done.5 = f32[2048,64]{0,1:T(8,128)S(1)} collective-permute-done((f32[2048,64]{0,1:T(8,128)S(1)}, f32[2048,64]{0,1:T(8,128)S(1)}, u32[]{:S(2)}, u32[]{:S(2)}) %collective-permute-start.5) | collective-permute-done | bytes 524320 | tf_op jit(solution)/shard_map/ppermute | solution.py:132
  322.5 0.8 copy-done.39
  323.3 1.3 copy.138
  324.6 1.3 copy.139
  325.9 1.3 copy.106
  327.2 1.3 copy.105
  328.4 1.1 add.127
  329.5 1.1 add.126
  330.6 3.9 pad_maximum_fusion.6
  334.5 130.2 %all-reduce.5.cloned.1.call-done = (f32[2048,512]{1,0:T(8,128)}, f32[2048,64]{0,1:T(8,128)}) async-done(((f32[2048,512]{1,0:T(8,128)}, f32[2048,64]{0,1:T(8,128)}), (f32[2048,512]{1,0:T(8,128)}, f32[2048,64]{0,1:T(8,128)})) %all-reduce.5.cloned.1.call-update) | async-done | bytes 4718608 | tf_op jit(solution)/shard_map/psum | solution.py:135
  464.8 27.4 %all-reduce.7.cloned.1.call-done = (f32[512,2,128]{2,1,0:T(2,128)}, f32[512,2,128]{2,1,0:T(2,128)}) async-done(((f32[512,2,128]{2,1,0:T(2,128)}, f32[512,2,128]{2,1,0:T(2,128)}), (f32[512,2,128]{2,1,0:T(2,128)}, f32[512,2,128]{2,1,0:T(2,128)})) %all-reduce.7.cloned.1.call-update) | async-done | bytes 1048592 | tf_op jit(solution)/shard_map/psum | solution.py:137
  492.2 4.7 copy.211
  496.9 0.8 copy.212
  497.7 0.8 copy.213
  498.5 0.8 copy.214
  (95 shorter events, 1.4 us)
Async XLA Ops:
  7.2 9.6 %copy-start.21 = (bf16[2048,2,192]{0,2,1:T(8,128)(2,1)S(1)}, bf16[2048,2,192]{0,2,1:T(8,128)(2,1)}, u32[]{:S(2)}) copy-start(bf16[2048,2,192]{0,2,1:T(8,128)(2,1)} %param.12) | copy-start | bytes 4718596
  7.2 457.6 %all-reduce.5.cloned.1.call-start = ((), (), s32[]{:S(2)}) async-start(), calls=%async_computation | async-start | bytes 9437184 | tf_op jit(solution)/shard_map/psum | solution.py:135
  7.2 75.0 %collective-permute-start.1 = (bf16[2048,64]{0,1:T(8,128)(2,1)}, bf16[2048,64]{0,1:T(8,128)(2,1)}, u32[]{:S(2)}, u32[]{:S(2)}) collective-permute-start(bf16[2048,64]{0,1:T(8,128)(2,1)} %param.11), channel_id=1, source_target_pairs={{0,1},{1,0},{2,3},{3,2},{4,5},{5,4},{6,7},{7,6},{8,9},{9,8},{10,11... | collective-permute-start | bytes 786440 | tf_op jit(solution)/shard_map/while/body/eval_jaxpr/ppermute | solution.py:91
  8.7 73.6 %collective-permute-start = (bf16[2048,512]{1,0:T(8,128)(2,1)}, bf16[2048,512]{1,0:T(8,128)(2,1)}, u32[]{:S(2)}, u32[]{:S(2)}) collective-permute-start(bf16[2048,512]{1,0:T(8,128)(2,1)} %param.10), channel_id=1, source_target_pairs={{0,1},{1,0},{2,3},{3,2},{4,5},{5,4},{6,7},{7,6},{8,9},{9,8},{10,11... | collective-permute-start | bytes 6291464 | tf_op jit(solution)/shard_map/while/body/eval_jaxpr/ppermute | solution.py:90
  11.1 54.3 %copy-start.23 = (bf16[2048,2,128]{2,0,1:T(8,128)(2,1)}, bf16[2048,2,128]{2,0,1:T(8,128)(2,1)S(1)}, u32[]{:S(2)}) copy-start(bf16[2048,2,128]{2,0,1:T(8,128)(2,1)S(1)} %convolution_convert_fusion.11) | copy-start | bytes 3145732
  13.8 3.0 copy-start.7
  16.7 13.2 %copy-start.36 = (bf16[2048,64]{0,1:T(8,128)(2,1)S(1)}, bf16[2048,64]{0,1:T(8,128)(2,1)}, u32[]{:S(2)}) copy-start(bf16[2048,64]{0,1:T(8,128)(2,1)} %param.11) | copy-start | bytes 786436
  65.4 15.5 %slice-start.4 = ((bf16[2048,2,192]{0,2,1:T(8,128)(2,1)}), bf16[2048,2,128]{0,2,1:T(8,128)(2,1)S(1)}, s32[]{:S(2)}) async-start(bf16[2048,2,192]{0,2,1:T(8,128)(2,1)} %param.12), calls=%async_computation.6 | async-start | bytes 2097152
  65.4 16.9 %copy-start.19 = (bf16[512,2,128]{2,1,0:T(2,128)(2,1)S(1)}, bf16[512,2,128]{2,1,0:T(2,128)(2,1)}, u32[]{:S(2)}) copy-start(bf16[512,2,128]{2,1,0:T(2,128)(2,1)} %param.15) | copy-start | bytes 786436
  82.3 56.0 %copy-start.3 = (bf16[2048,2,128]{2,1,0:T(2,128)(2,1)S(1)}, bf16[2048,2,128]{2,1,0:T(2,128)(2,1)}, u32[]{:S(2)}) copy-start(bf16[2048,2,128]{2,1,0:T(2,128)(2,1)} %param.13) | copy-start | bytes 3145732
  136.6 1.7 copy-start.25
  138.2 14.3 %copy-start.26 = (f32[2048,2,128]{2,1,0:T(2,128)S(1)}, f32[2048,2,128]{2,1,0:T(2,128)}, u32[]{:S(2)}) copy-start(f32[2048,2,128]{2,1,0:T(2,128)} %copy-done.25) | copy-start | bytes 6291460
  138.2 14.3 %copy-start.34 = (f32[2048,2]{1,0:T(8,128)S(1)}, f32[2048,2]{1,0:T(8,128)}, u32[]{:S(2)}) copy-start(f32[2048,2]{1,0:T(8,128)} %copy.80) | copy-start | bytes 49156
  138.2 44.8 %copy-start.24 = (bf16[2048,2,128]{2,0,1:T(8,128)(2,1)S(1)}, bf16[2048,2,128]{2,0,1:T(8,128)(2,1)}, u32[]{:S(2)}) copy-start(bf16[2048,2,128]{2,0,1:T(8,128)(2,1)} %copy-done.23) | copy-start | bytes 3145732
  182.0 1.0 copy-start.13
  201.6 18.4 %slice-start = ((s8[16777216]{0:T(1024)(128)(4,1)}), s8[4194304]{0:T(1024)(128)(4,1)S(1)}, s32[]{:S(2)}) async-start(s8[16777216]{0:T(1024)(128)(4,1)} %bitcast.245), calls=%async_computation.2 | async-start | bytes 8388608
  201.6 18.4 %slice-start.1 = ((s8[16777216]{0:T(1024)(128)(4,1)}), s8[4194304]{0:T(1024)(128)(4,1)S(1)}, s32[]{:S(2)}) async-start(s8[16777216]{0:T(1024)(128)(4,1)} %bitcast.245), calls=%async_computation.3 | async-start | bytes 8388608
  201.6 18.4 %slice-start.2 = ((s8[16777216]{0:T(1024)(128)(4,1)}), s8[4194304]{0:T(1024)(128)(4,1)S(1)}, s32[]{:S(2)}) async-start(s8[16777216]{0:T(1024)(128)(4,1)} %bitcast.245), calls=%async_computation.4 | async-start | bytes 8388608
  213.3 2.2 copy-start.17
  213.3 6.7 %slice-start.3 = ((s8[16777216]{0:T(1024)(128)(4,1)}), s8[4194304]{0:T(1024)(128)(4,1)S(1)}, s32[]{:S(2)}) async-start(s8[16777216]{0:T(1024)(128)(4,1)} %bitcast.245), calls=%async_computation.5 | async-start | bytes 8388608
  213.3 6.7 %copy-start.22 = (bf16[2048,2,192]{0,2,1:T(8,128)(2,1)S(1)}, bf16[2048,2,192]{0,2,1:T(8,128)(2,1)}, u32[]{:S(2)}) copy-start(bf16[2048,2,192]{0,2,1:T(8,128)(2,1)} %param.12) | copy-start | bytes 4718596
  216.2 9.6 %copy-start.37 = (bf16[2048,64]{0,1:T(8,128)(2,1)S(1)}, bf16[2048,64]{0,1:T(8,128)(2,1)}, u32[]{:S(2)}) copy-start(bf16[2048,64]{0,1:T(8,128)(2,1)} %param.11) | copy-start | bytes 786436
  216.2 20.5 %collective-permute-start.2 = (f32[2048,512]{1,0:T(8,128)S(1)}, f32[2048,512]{1,0:T(8,128)}, u32[]{:S(2)}, u32[]{:S(2)}) collective-permute-start(f32[2048,512]{1,0:T(8,128)S(1)} %bitcast_add_fusion.7), channel_id=1, source_target_pairs={{0,1},{1,0},{2,3},{3,2},{4,5},{5,4},{6,7},{7,6},{8,9},{9,8},{10,11... | collective-permute-start | bytes 12582920 | tf_op jit(solution)/shard_map/while/body/eval_jaxpr/ppermute | solution.py:114
  225.2 4.7 copy-start.8
  225.2 11.5 %collective-permute-start.3 = (f32[2048,64]{0,1:T(8,128)S(1)}, f32[2048,64]{0,1:T(8,128)}, u32[]{:S(2)}, u32[]{:S(2)}) collective-permute-start(f32[2048,64]{0,1:T(8,128)S(1)} %convolution_bitcast_fusion.7), channel_id=1, source_target_pairs={{0,1},{1,0},{2,3},{3,2},{4,5},{5,4},{6,7},{7,6},{8,9},{9,8},{10,11... | collective-permute-start | bytes 1572872 | tf_op jit(solution)/shard_map/while/body/eval_jaxpr/ppermute | solution.py:115
  229.8 3.8 copy-start.9
  229.8 5.3 %copy-start.20 = (bf16[2048,2,128]{2,0,1:T(8,128)(2,1)S(1)}, bf16[2048,2,128]{2,0,1:T(8,128)(2,1)}, u32[]{:S(2)}) copy-start(bf16[2048,2,128]{2,0,1:T(8,128)(2,1)} %fusion.163) | copy-start | bytes 3145732
  233.7 3.1 copy-start.2
  233.7 3.1 copy-start.4
  248.1 6.9 %copy-start.28 = (bf16[1024,2,128]{2,0,1:T(8,128)(2,1)}, bf16[1024,2,128]{2,0,1:T(8,128)(2,1)S(1)}, u32[]{:S(2)}) copy-start(bf16[1024,2,128]{2,0,1:T(8,128)(2,1)S(1)} %convolution_convert_fusion.5) | copy-start | bytes 1572868 | tf_op jit(solution)/shard_map/while/body/eval_jaxpr/cond
  251.3 3.6 copy-start.16
  282.9 6.4 %copy-start.1 = (bf16[2048,2,1024]{0,2,1:T(8,128)(2,1)S(1)}, bf16[2048,2,1024]{0,2,1:T(8,128)(2,1)}, u32[]{:S(2)}) copy-start(bf16[2048,2,1024]{0,2,1:T(8,128)(2,1)} %fusion.49) | copy-start | bytes 25165828 | tf_op jit(solution)/shard_map/while/body/eval_jaxpr/cond
  282.9 6.4 %copy-start.12 = (bf16[2048,2,128]{2,0,1:T(8,128)(2,1)S(1)}, bf16[2048,2,128]{2,0,1:T(8,128)(2,1)}, u32[]{:S(2)}) copy-start(bf16[2048,2,128]{2,0,1:T(8,128)(2,1)} %get-tuple-element.238) | copy-start | bytes 3145732 | tf_op jit(solution)/shard_map/while/body/eval_jaxpr/cond
  282.9 8.7 %copy-start.29 = (bf16[1024,2,128]{2,0,1:T(8,128)(2,1)S(1)}, bf16[1024,2,128]{2,0,1:T(8,128)(2,1)}, u32[]{:S(2)}) copy-start(bf16[1024,2,128]{2,0,1:T(8,128)(2,1)} %copy-done.28) | copy-start | bytes 1572868 | tf_op jit(solution)/shard_map/while/body/eval_jaxpr/cond
  291.7 2.7 copy-start.6
  294.4 3.6 copy-start.38
  294.4 6.3 %copy-start.32 = (bf16[1024,2,128]{2,0,1:T(8,128)(2,1)S(1)}, bf16[1024,2,128]{2,0,1:T(8,128)(2,1)}, u32[]{:S(2)}) copy-start(bf16[1024,2,128]{2,0,1:T(8,128)(2,1)} %fusion.60) | copy-start | bytes 1572868 | tf_op jit(solution)/shard_map/while/body/eval_jaxpr/cond
  294.4 8.8 %copy-start.31 = (bf16[512,2,128]{2,1,0:T(2,128)(2,1)S(1)}, bf16[512,2,128]{2,1,0:T(2,128)(2,1)}, u32[]{:S(2)}) copy-start(bf16[512,2,128]{2,1,0:T(2,128)(2,1)} %get-tuple-element.350) | copy-start | bytes 786436 | tf_op jit(solution)/shard_map/while/body/eval_jaxpr/cond
  298.0 7.8 %copy-start.27 = (f32[1024,512]{1,0:T(8,128)S(1)}, f32[1024,512]{1,0:T(8,128)}, u32[]{:S(2)}) copy-start(f32[1024,512]{1,0:T(8,128)} %slice.76) | copy-start | bytes 6291460 | tf_op jit(solution)/shard_map/while/body/eval_jaxpr/cond
  308.5 13.9 %collective-permute-start.4 = (f32[2048,512]{1,0:T(8,128)}, f32[2048,512]{1,0:T(8,128)}, u32[]{:S(2)}, u32[]{:S(2)}) collective-permute-start(f32[2048,512]{1,0:T(8,128)} %get-tuple-element.367), channel_id=1, source_target_pairs={{0,1},{1,0},{2,3},{3,2},{4,5},{5,4},{6,7},{7,6},{8,9},{9,8},{10,11... | collective-permute-start | bytes 12582920 | tf_op jit(solution)/shard_map/ppermute | solution.py:131
  314.9 7.5 %collective-permute-start.5 = (f32[2048,64]{0,1:T(8,128)S(1)}, f32[2048,64]{0,1:T(8,128)S(1)}, u32[]{:S(2)}, u32[]{:S(2)}) collective-permute-start(f32[2048,64]{0,1:T(8,128)S(1)} %get-tuple-element.368), channel_id=1, source_target_pairs={{0,1},{1,0},{2,3},{3,2},{4,5},{5,4},{6,7},{7,6},{8,9},{9,8},{10,11... | collective-permute-start | bytes 1572872 | tf_op jit(solution)/shard_map/ppermute | solution.py:132
  322.5 0.8 copy-start.39
  323.3 168.9 %all-reduce.7.cloned.1.call-start = ((), (), s32[]{:S(2)}) async-start(), calls=%async_computation.1 | async-start | bytes 2097152 | tf_op jit(solution)/shard_map/psum | solution.py:137
  464.8 32.2 %copy-start.40 = (f32[2048,64]{0,1:T(8,128)S(1)}, f32[2048,64]{0,1:T(8,128)}, u32[]{:S(2)}) copy-start(f32[2048,64]{0,1:T(8,128)} %get-tuple-element.431) | copy-start | bytes 1572868
  492.2 5.5 %copy-start.42 = (f32[512,2,128]{2,1,0:T(2,128)S(1)}, f32[512,2,128]{2,1,0:T(2,128)}, u32[]{:S(2)}) copy-start(f32[512,2,128]{2,1,0:T(2,128)} %get-tuple-element.432) | copy-start | bytes 1572868
  492.2 6.3 %copy-start.41 = (f32[512,2,128]{2,1,0:T(2,128)S(1)}, f32[512,2,128]{2,1,0:T(2,128)}, u32[]{:S(2)}) copy-start(f32[512,2,128]{2,1,0:T(2,128)} %get-tuple-element.433) | copy-start | bytes 1572868
Sparse Core Ops, SparseCore 0:
  323.4 141.3 all-reduce.4
  467.8 24.3 all-reduce.6
where the time goes:
time: 515 us; the launch traced here: 507 us
  matrix products  209 us (41%)
  waiting for transfers between devices  165 us (32%)
  other arithmetic  62.1 us (12%)
  local copies, waits for them, and re-layouts  28.3 us (5%)
  loops' own time  15 us (3%)
  between operations  14.9 us (3%)
  starting transfers between devices  12.5 us (2%)
    psum x1, waiting for transfers between devices, device_fn(): lax.psum(dc_acc, 'tp')  130 us
    dot_general x3, matrix products, block_scores(): jnp.einsum('qhd,kd->qhk', q_rope, rope_blk, preferred_element_type=jnp.fl...  45.3 us
    reduce_sum x1, other arithmetic, device_fn(): d_dot = jnp.sum(d_out.astype(jnp.float32) * out_wide, axis=-1)  29.5 us
    dot_general x2, matrix products, backward_block(): jnp.einsum('qhd,khd->qhk', d_out, v_blk, preferred_element_type=jnp.float32)  28.9 us
    psum x1, waiting for transfers between devices, device_fn(): lax.psum(dw_k, 'cp')  27.4 us
    dot_general x3, matrix products, block_scores(): jnp.einsum('qhd,khd->qhk', q_nope, knope_blk, preferred_element_type=jnp....  27.2 us
    dot_general x2, matrix products, forward_update(): jnp.einsum('qhk,khd->qhd', prob_blk.astype(jnp.bfloat16), v_blk, preferre...  24.2 us
    dot_general x2, matrix products, backward_block(): jnp.einsum('qhk,qhd->khd', prob_blk.astype(jnp.bfloat16), d_out, preferre...  23.2 us
  transfers between devices with their start and end apart: 8, of which 3 were waited for; matrix products, arithmetic and copies ran while one was open for 20% of the time, Pallas kernels for 0%

commit v1 on v0

v1 whole, which is shorter than its diff:
```python
import functools
import math

import jax
import jax.numpy as jnp
from jax import lax
from jax.experimental import pallas as pl
from jax.experimental.pallas import tpu as pltpu
from jax.sharding import PartitionSpec as P

BF = jnp.bfloat16
F32 = jnp.float32
NEG_BIG = -1.0e30
LOG2E = math.log2(math.e)


def mm(a, b):
    return lax.dot_general(a, b, (((1,), (0,)), ((), ())), preferred_element_type=F32)


def mm_nt(a, b):
    return lax.dot_general(a, b, (((1,), (1,)), ((), ())), preferred_element_type=F32)


def mm_tn(a, b):
    return lax.dot_general(a, b, (((0,), (0,)), ((), ())), preferred_element_type=F32)


def fwd_kernel(blk, dn, dv, c_ref, r_ref, q_ref, do_ref, wuk_ref, wuv_ref,
               o_ref, lse_ref, dd_ref, kc_ref, v_ref, kt_ref, vt_scr, kc_scr, m_scr, l_scr, acc_scr):
    i = pl.program_id(0)
    qk = q_ref.shape[1]
    scale2 = (qk ** -0.5) * LOG2E
    kb = mm(c_ref[...], wuk_ref[...]).astype(BF)
    vb = mm(c_ref[...], wuv_ref[...])
    rows = pl.ds(pl.multiple_of(i * blk, blk), blk)
    kc_scr[rows, :dn] = kb
    kc_scr[rows, dn:] = r_ref[...]
    kc_ref[:, :dn] = kb
    kc_ref[:, dn:] = r_ref[...]
    v_ref[...] = vb.astype(BF)
    vt_scr[i] = vb.T.astype(BF)
    kcv = kc_scr[rows, :]
    kt_ref[...] = kcv.astype(F32).T.astype(BF)[None]

    def update(j, masked, first):
        ks = pl.ds(pl.multiple_of(j * blk, blk), blk)
        s = mm_nt(kc_scr[ks, :], q_ref[...])
        if masked:
            kpos = lax.broadcasted_iota(jnp.int32, (blk, blk), 0)
            qpos = lax.broadcasted_iota(jnp.int32, (blk, blk), 1)
            s = jnp.where(kpos <= qpos, s, NEG_BIG)
        m_blk = jnp.max(s, axis=0, keepdims=True)
        if first:
            m_new = m_blk
        else:
            m_new = jnp.maximum(m_scr[...], m_blk)
        e = jnp.exp2(s * scale2 - m_new * scale2)
        l_blk = jnp.sum(e, axis=0, keepdims=True)
        o_blk = mm(vt_scr[j], e.astype(BF))
        if first:
            l_scr[...] = l_blk
            acc_scr[...] = o_blk
        else:
            alpha = jnp.exp2((m_scr[...] - m_new) * scale2)
            l_scr[...] = l_scr[...] * alpha + l_blk
            acc_scr[...] = acc_scr[...] * alpha + o_blk
        m_scr[...] = m_new

    update(i, True, True)

    def body(j, _):
        update(j, False, False)
        return _

    lax.fori_loop(0, i, body, 0)
    ot = acc_scr[...] / l_scr[...]
    o_ref[...] = ot.T.astype(BF)
    dot_t = do_ref[...].astype(F32).T
    dd_ref[...] = jnp.sum(dot_t * ot, axis=0, keepdims=True)
    lse_ref[...] = m_scr[...] * scale2 + jnp.log2(l_scr[...])


def bwd_kernel(blk, nb, dn, dv, q_ref, do_ref, lse_ref, dd_ref, kc_ref, v_ref, kt_ref, c_ref, wuk_ref, wuv_ref,
               dq_ref, dc_ref, dr_ref, dwk_ref, dwv_ref, dqt_scr, dk_scr, dv_scr):
    step = pl.program_id(0)
    j = nb - 1 - step
    qk = q_ref.shape[1]
    scale = qk ** -0.5
    scale2 = scale * LOG2E
    kc = kc_ref[...]
    v = v_ref[...]
    kt = kt_ref[0]

    def pair(i, masked, first):
        qs = pl.ds(pl.multiple_of(i * blk, blk), blk)
        q = q_ref[qs, :]
        do = do_ref[qs, :]
        s = mm_nt(kc, q)
        p = jnp.exp2(s * scale2 - lse_ref[:, qs])
        if masked:
            kpos = lax.broadcasted_iota(jnp.int32, (blk, blk), 0)
            qpos = lax.broadcasted_iota(jnp.int32, (blk, blk), 1)
            p = jnp.where(kpos <= qpos, p, 0.0)
        dp = mm_nt(v, do)
        ds = (p * (dp - dd_ref[:, qs])).astype(BF)
        dq_blk = mm(kt, ds)
        dk_blk = mm(ds, q)
        dv_blk = mm(p.astype(BF), do)
        if first:
            dqt_scr[i] = dq_blk
            dk_scr[...] = dk_blk
            dv_scr[...] = dv_blk
        else:
            dqt_scr[i] += dq_blk
            dk_scr[...] += dk_blk
            dv_scr[...] += dv_blk

    pair(j, True, True)

    def body(i, _):
        pair(i, False, False)
        return _

    lax.fori_loop(j + 1, nb, body, 0)
    dk = dk_scr[...] * scale
    dkb = dk[:, :dn].astype(BF)
    dvb = dv_scr[...].astype(BF)
    dr_ref[...] = dk[:, dn:]
    dc_ref[...] = mm_nt(dkb, wuk_ref[...]) + mm_nt(dvb, wuv_ref[...])
    dwk = mm_tn(c_ref[...], dkb)
    dwv = mm_tn(c_ref[...], dvb)

    @pl.when(step == 0)
    def _():
        dwk_ref[...] = dwk
        dwv_ref[...] = dwv

    @pl.when(step > 0)
    def _():
        dwk_ref[...] += dwk
        dwv_ref[...] += dwv

    @pl.when(step == nb - 1)
    def _():
        def fin(i, _):
            qs = pl.ds(pl.multiple_of(i * blk, blk), blk)
            dq_ref[qs, :] = (dqt_scr[i] * scale).T
            return _
        lax.fori_loop(0, nb, fin, 0)


def attention(c, r, q, do, wuk, wuv, blk=512, vmem=60 * 2**20):
    t, rank = c.shape
    dr = r.shape[1]
    qk = q.shape[1]
    dn = wuk.shape[1]
    dv = wuv.shape[1]
    nb = t // blk
    row = lambda i: (i, 0)
    col = lambda i: (0, i)
    full = lambda i: (0, 0)
    sds = jax.ShapeDtypeStruct
    o, lse, dd, kc, v, kt = pl.pallas_call(
        functools.partial(fwd_kernel, blk, dn, dv),
        grid=(nb,),
        in_specs=[pl.BlockSpec((blk, rank), row), pl.BlockSpec((blk, dr), row), pl.BlockSpec((blk, qk), row),
                  pl.BlockSpec((blk, dv), row), pl.BlockSpec((rank, dn), full), pl.BlockSpec((rank, dv), full)],
        out_specs=[pl.BlockSpec((blk, dv), row), pl.BlockSpec((1, blk), col), pl.BlockSpec((1, blk), col),
                   pl.BlockSpec((blk, qk), row), pl.BlockSpec((blk, dv), row),
                   pl.BlockSpec((1, qk, blk), lambda i: (i, 0, 0))],
        out_shape=[sds((t, dv), BF), sds((1, t), F32), sds((1, t), F32), sds((t, qk), BF), sds((t, dv), BF),
                   sds((nb, qk, blk), BF)],
        scratch_shapes=[pltpu.VMEM((nb, dv, blk), BF), pltpu.VMEM((t, qk), BF), pltpu.VMEM((1, blk), F32),
                        pltpu.VMEM((1, blk), F32), pltpu.VMEM((dv, blk), F32)],
        compiler_params=pltpu.CompilerParams(vmem_limit_bytes=vmem),
        name="mla_fwd",
    )(c, r, q, do, wuk, wuv)
    rrow = lambda s: (nb - 1 - s, 0)
    dq, dc, drk, dwk, dwv = pl.pallas_call(
        functools.partial(bwd_kernel, blk, nb, dn, dv),
        grid=(nb,),
        in_specs=[pl.BlockSpec((t, qk), full), pl.BlockSpec((t, dv), full), pl.BlockSpec((1, t), full),
                  pl.BlockSpec((1, t), full), pl.BlockSpec((blk, qk), rrow), pl.BlockSpec((blk, dv), rrow),
                  pl.BlockSpec((1, qk, blk), lambda s: (nb - 1 - s, 0, 0)), pl.BlockSpec((blk, rank), rrow),
                  pl.BlockSpec((rank, dn), full), pl.BlockSpec((rank, dv), full)],
        out_specs=[pl.BlockSpec((t, qk), full), pl.BlockSpec((blk, rank), rrow), pl.BlockSpec((blk, dr), rrow),
                   pl.BlockSpec((rank, dn), full), pl.BlockSpec((rank, dv), full)],
        out_shape=[sds((t, qk), F32), sds((t, rank), F32), sds((t, dr), F32), sds((rank, dn), F32), sds((rank, dv), F32)],
        scratch_shapes=[pltpu.VMEM((nb, qk, blk), F32), pltpu.VMEM((blk, qk), F32), pltpu.VMEM((blk, dv), F32)],
        compiler_params=pltpu.CompilerParams(vmem_limit_bytes=vmem),
        name="mla_bwd",
    )(q, do, lse, dd, kc, v, kt, c, wuk, wuv)
    return o, dq, dc, drk, dwk, dwv


PIECE = 1024
LANES = 128


def ar_kernel(strides, side, dc_ref, dr_ref, dco_ref, dro_ref, acc, d2d, *scr):
    rbufs, (loc_sem, send_sem, recv_sem) = scr[:-3], scr[-3:]
    tp = lax.axis_index("tp")
    cp = lax.axis_index("cp")
    n_half = 2
    cols = dco_ref.shape[1] // LANES
    n_units = n_half * cols + 1
    coord = [lax.rem(tp // st, side) for st in strides]

    def nbr(a, off):
        return tp + (lax.rem(coord[a] + off + side, side) - coord[a]) * strides[a]

    barrier = pltpu.get_barrier_semaphore()
    for a in range(3):
        for off in (1, side - 1):
            pl.semaphore_signal(barrier, inc=1, device_id={"tp": nbr(a, off)}, device_id_type=pl.DeviceIdType.MESH)
    pl.semaphore_signal(barrier, inc=1, device_id={"cp": 1 - cp}, device_id_type=pl.DeviceIdType.MESH)
    pl.semaphore_wait(barrier, 7)

    def part(u, owner):
        if u == n_units - 1:
            return dr_ref.at[owner]
        w, b = divmod(u, cols)
        piece = owner if w == 0 else 3 - owner
        return dc_ref.at[pl.ds(pl.multiple_of(piece * PIECE, PIECE), PIECE), pl.ds(b * LANES, LANES)]

    def out_at(u, start, n):
        if u == n_units - 1:
            return dro_ref.at[pl.ds(start, n), :]
        w, b = divmod(u, cols)
        return dco_ref.at[pl.ds(pl.multiple_of(w * PIECE + start, 8), n), pl.ds(b * LANES, LANES)]

    sends = []

    def copy(src, dst, u, k, dev):
        cpy = pltpu.make_async_remote_copy(src_ref=src, dst_ref=dst, send_sem=send_sem.at[u, k], recv_sem=recv_sem.at[u, k],
                                           device_id=dev, device_id_type=pl.DeviceIdType.MESH)
        cpy.start()
        sends.append(cpy)
        return cpy

    first = []
    for u in range(n_units):
        far = copy(part(u, 1 - cp), d2d.at[u], u, 0, {"cp": 1 - cp})
        near = pltpu.make_async_copy(part(u, cp), acc.at[u], loc_sem.at[u])
        near.start()
        first.append((near, far))

    def unit(u):
        axes = [(u + t) % 3 for t in range(3)]
        near, far = first[u]
        near.wait()
        far.wait_recv()
        acc[u] = acc[u] + d2d[u]
        k = 1
        base, size = 0, PIECE
        levels = []
        for t, a in enumerate(axes):
            n = size // side
            h = n // 2
            i = coord[a]
            r1, r2 = rbufs[2 * t], rbufs[2 * t + 1]
            at = lambda o, extra=0: pl.multiple_of(base + lax.rem(i + o, side) * n + extra, 8)
            fwd, bwd = {"tp": nbr(a, 1)}, {"tp": nbr(a, side - 1)}
            opp = at(2)
            c1 = copy(acc.at[u, pl.ds(opp, h)], r1.at[u, 0], u, k, fwd)
            c2 = copy(acc.at[u, pl.ds(at(2, h), h)], r1.at[u, 1], u, k + 1, bwd)
            yield
            c1.wait_recv()
            p1 = at(1)
            acc[u, pl.ds(p1, h)] = acc[u, pl.ds(p1, h)] + r1[u, 0]
            c3 = copy(acc.at[u, pl.ds(p1, n)], r2.at[u, 0], u, k + 2, fwd)
            c2.wait_recv()
            m1 = at(side - 1)
            m1h = at(side - 1, h)
            acc[u, pl.ds(m1h, h)] = acc[u, pl.ds(m1h, h)] + r1[u, 1]
            c4 = copy(acc.at[u, pl.ds(m1, n)], r2.at[u, 1], u, k + 3, bwd)
            yield
            c3.wait_recv()
            c4.wait_recv()
            own = at(0)
            total = acc[u, pl.ds(own, n)] + r2[u, 0] + r2[u, 1]
            if t < 2:
                acc[u, pl.ds(own, n)] = total
            else:
                out_at(u, own, n)[...] = total
            levels.append((base, n, a))
            base, size = own, n
            k += 4
        for base, n, a in reversed(levels):
            h = n // 2
            i = coord[a]
            at = lambda o, extra=0: pl.multiple_of(base + lax.rem(i + o, side) * n + extra, 8)
            fwd, bwd = {"tp": nbr(a, 1)}, {"tp": nbr(a, side - 1)}
            mine = out_at(u, at(0), n)
            c1 = copy(mine, mine, u, k, fwd)
            c2 = copy(mine, mine, u, k + 1, bwd)
            yield
            c1.wait_recv()
            got = out_at(u, at(side - 1), h)
            c3 = copy(got, got, u, k + 2, fwd)
            c2.wait_recv()
            got = out_at(u, at(1, h), h)
            c4 = copy(got, got, u, k + 3, bwd)
            yield
            c3.wait_recv()
            c4.wait_recv()
            k += 4

    live = [unit(u) for u in range(n_units)]
    while live:
        nxt = []
        for g in live:
            try:
                next(g)
                nxt.append(g)
            except StopIteration:
                pass
        live = nxt
    for c in sends:
        c.wait_send()


def all_reduce(dc, drp, side=4, vmem=60 * 2**20):
    rows = dc.shape[0] // 2
    cols = dc.shape[1] // LANES
    nu = 2 * cols + 1
    bufs = []
    size = PIECE
    for _ in range(3):
        n = size // side
        bufs += [pltpu.VMEM((nu, 2, n // 2, LANES), F32), pltpu.VMEM((nu, 2, n, LANES), F32)]
        size = n
    return pl.pallas_call(
        functools.partial(ar_kernel, (1, side, side * side), side),
        in_specs=[pl.BlockSpec(memory_space=pl.ANY)] * 2,
        out_specs=[pl.BlockSpec(memory_space=pltpu.VMEM)] * 2,
        out_shape=[jax.ShapeDtypeStruct((rows, dc.shape[1]), F32), jax.ShapeDtypeStruct((PIECE, LANES), F32)],
        scratch_shapes=[pltpu.VMEM((nu, PIECE, LANES), F32), pltpu.VMEM((nu, PIECE, LANES), F32)] + bufs
        + [pltpu.SemaphoreType.DMA((nu,)), pltpu.SemaphoreType.DMA((nu, 25)), pltpu.SemaphoreType.DMA((nu, 25))],
        compiler_params=pltpu.CompilerParams(collective_id=0, has_side_effects=True, vmem_limit_bytes=vmem),
        name="grad_sum",
    )(dc, drp)


def solution(mesh):
    n_cp = mesh.shape['cp']
    side = round(mesh.shape['tp'] ** (1 / 3))
    swap = [(d, n_cp - 1 - d) for d in range(n_cp)]
    seq_spec = P(('dp', 'cp'), None)
    head_spec = P(('dp', 'cp'), 'tp', None)
    weight_spec = P(None, 'tp', None)
    grad_spec = P('dp', 'tp', None)

    def device_fn(c_latent, k_rope, q_heads, d_out, w_uk, w_uv):
        me = lax.axis_index('cp')
        other = 1 - me
        half = c_latent.shape[0] // 2
        pick = lambda x, h: lax.dynamic_index_in_dim(x, h, 1, keepdims=False)
        xchg = lambda x: lax.ppermute(x, 'cp', swap)

        def natural(own, far):
            outer = jnp.where(me == 0, own, far)
            inner = jnp.where(me == 0, far, own)
            return jnp.concatenate([outer[:half], inner, outer[half:]], axis=0)

        def unnatural(full):
            outer = jnp.concatenate([full[:half], full[3 * half:]], axis=0)
            inner = full[half:3 * half]
            return jnp.where(me == 0, outer, inner), jnp.where(me == 0, inner, outer)

        c = natural(c_latent, xchg(c_latent))
        r = natural(k_rope, xchg(k_rope))
        q = natural(pick(q_heads, me), xchg(pick(q_heads, other)))
        do = natural(pick(d_out, me), xchg(pick(d_out, other)))
        o, dq, dc, dr, dwk, dwv = attention(c, r, q, do, pick(w_uk, me), pick(w_uv, me))
        drp = jnp.stack([jnp.concatenate([dr[:half], dr[3 * half:]], axis=1),
                         jnp.concatenate([dr[half:2 * half], dr[2 * half:3 * half]], axis=1)])
        dc_sum, drp_sum = all_reduce(dc, drp, side)
        dr_sum = jnp.concatenate([drp_sum[:, :64], drp_sum[:, 64:]], axis=0)

        def pair(own, far):
            return jnp.where(me == 0, jnp.stack([own, far], axis=1), jnp.stack([far, own], axis=1))

        o_own, o_far = unnatural(o)
        dq_own, dq_far = unnatural(dq)
        return (pair(o_own, xchg(o_far)), pair(dq_own, xchg(dq_far)), dc_sum, dr_sum,
                pair(dwk, xchg(dwk)), pair(dwv, xchg(dwv)))

    return jax.shard_map(device_fn, mesh=mesh,
                         in_specs=(seq_spec, seq_spec, head_spec, head_spec, weight_spec, weight_spec),
                         out_specs=(head_spec, head_spec, seq_spec, seq_spec, grad_spec, grad_spec),
                         check_vma=False)
```

time: 515 us -> 222 us (0.43)
  the two profiles are of different devices: /device:TPU:1 before, /device:TPU:0 now
where the time goes in v1:
time: 222 us; the launch traced here: 221 us
  Pallas kernels  149 us (67%)
  local copies, waits for them, and re-layouts  45.2 us (20%)
  other arithmetic  23.5 us (11%)
  starting transfers between devices  2.25 us (1%)
    pallas_call x1, Pallas kernels, all_reduce(): pl.pallas_call(functools.partial(ar_kernel, (1, side, side * side), side)...  70.3 us
    pallas_call x1, Pallas kernels, attention(): pl.pallas_call(functools.partial(bwd_kernel, blk, nb, dn, dv), grid=(nb,)...  47.8 us
    pallas_call x1, Pallas kernels, attention(): pl.pallas_call(functools.partial(fwd_kernel, blk, dn, dv), grid=(nb,), in...  31.4 us
    unnamed x18, local copies, waits for them, and re-layouts  27.3 us
    select_n x4, other arithmetic, pair(): jnp.where(me == 0, jnp.stack([own, far], axis=1), jnp.stack([far, own], a...  8.15 us
    dynamic_slice x4, local copies, waits for them, and re-layouts, device_fn(): pick = lambda x, h: lax.dynamic_index_in_dim(x, h, 1, keepdims=False)  6.66 us
    concatenate x4, other arithmetic, natural(): return jnp.concatenate([outer[:half], inner, outer[half:]], axis=0)  6.06 us
    select_n x4, other arithmetic, natural(): inner = jnp.where(me == 0, far, own)  4.89 us
  transfers between devices with their start and end apart: 8, of which 0 were waited for; matrix products, arithmetic and copies ran while one was open for 19% of the time, Pallas kernels for 53%

profile of v1, /device:TPU:0, one launch (start us, length us, event | category | flops | bytes accessed | tf_op | source)
XLA Modules:
  0.0 221.2 jit_solution(8029799588131990093)
XLA Ops:
  0.6 0.0 copy-start
  0.6 1.3 copy.37
  2.0 0.1 collective-permute-start.1
  2.1 2.4 %constant_dynamic-slice_fusion.4 = (bf16[2048,1,192]{0,2,1:T(8,128)(2,1)S(1)}, bf16[2048,192]{0,1:T(8,128)(2,1)}) fusion(bf16[2048,2,192]{0,2,1:T(8,128)(2,1)} %param.8, s32[]{:T(128)S(6)} %select_n.116, s32[]{:T(128)S(6)} %select_n.117), kind=kLoop, calls=%fused_computation.35 | loop fusion | bytes 3145736 | tf_op jit(solution)/shard_map/jit(dynamic_index_in_dim)/dynamic_slice | solution.py:359
  4.5 0.5 collective-permute-start.2
  4.9 0.0 copy-done
  4.9 2.2 constant_dynamic-slice_fusion.3
  7.1 0.9 copy.65
  8.0 0.0 collective-permute-start.3
  8.0 0.5 collective-permute-start
  8.5 1.6 constant_dynamic-slice_fusion
  10.1 0.7 copy.66
  10.8 0.7 copy.67
  11.4 0.5 copy.39
  11.9 0.0 collective-permute-done.1
  12.0 1.1 broadcast_select_fusion.2
  13.1 1.2 pad_maximum_fusion.3.r_ref
  14.3 0.0 collective-permute-done.3
  14.3 1.1 broadcast_select_fusion.5
  15.5 1.1 pad_maximum_fusion.4.do_ref
  16.5 0.0 collective-permute-done.2
  16.5 1.4 copy.40
  18.0 0.1 bitcast_select_fusion
  18.1 0.1 fusion.4
  18.2 1.7 pad_maximum_fusion.1.q_ref
  19.9 0.0 collective-permute-done
  19.9 2.5 %broadcast_select_fusion = (bf16[2048,512]{1,0:T(8,128)(2,1)S(1)}, bf16[2048,512]{1,0:T(8,128)(2,1)S(1)}) fusion(bf16[2048,512]{1,0:T(8,128)(2,1)} %collective-permute-done, bf16[2048,512]{1,0:T(8,128)(2,1)} %param.6, pred[]{:T(512)S(6)} %eq.2), kind=kLoop, calls=%fused_computation.5 | loop fusion | flops 2097152 | bytes 8388609 | tf_op jit(solution)/shard_map/jit(_where)/select_n | solution.py:364
  22.4 0.1 fusion.2
  22.5 2.2 pad_maximum_fusion.c_ref
  24.7 31.4 %mla_fwd.1 = (bf16[4096,128]{1,0:T(8,128)(2,1)}, f32[1,4096]{1,0:T(1,128)}, f32[1,4096]{1,0:T(1,128)}, bf16[4096,192]{1,0:T(8,128)(2,1)}, bf16[4096,128]{1,0:T(8,128)(2,1)}, /*index=5*/bf16[8,192,512]{2,1,0:T(8,128)(2,1)}) custom-call(bf16[4096,512]{1,0:T(8,128)(2,1)} %pad_maximum_fusion.c_ref, bf16[4096,64]{1,0:T(8,128)(2,1)} %pad_maximum_fusion.3.r_ref, ...), custom_call_target="tpu_custom_call" | custom-call | tf_op jit(solution)/shard_map/mla_fwd/pallas_call | solution.py:164
  56.1 1.1 fusion.3
  57.1 1.2 select_bitcast_fusion.1
  58.4 0.1 collective-permute-start.4
  58.5 47.8 %mla_bwd.1 = (f32[4096,192]{1,0:T(8,128)}, f32[4096,512]{1,0:T(8,128)}, f32[4096,64]{1,0:T(8,128)}, f32[512,128]{1,0:T(8,128)}, f32[512,128]{1,0:T(8,128)}) custom-call(bf16[4096,192]{1,0:T(8,128)(2,1)} %pad_maximum_fusion.1.q_ref, bf16[4096,128]{1,0:T(8,128)(2,1)} %pad_maximum_fusion.4.do_ref, f32[1,4096]{1,0:T(1,128)} %get-tuple-element.20.lse_ref, ...), custom_call_target="tpu_custom_call" | custom-call | tf_op jit(solution)/shard_map/mla_bwd/pallas_call | solution.py:180
  106.3 0.6 collective-permute-start.6
  106.8 0.1 collective-permute-start.7
  106.9 1.8 fusion
  108.8 1.0 copy-done.1
  109.7 1.6 select_bitcast_fusion
  111.3 1.7 copy.46
  113.0 0.4 collective-permute-start.5
  113.4 1.7 fusion.1
  115.1 0.2 maximum_bitcast_fusion
  115.3 0.2 maximum_bitcast_fusion.1
  115.5 1.0 pad_maximum_fusion.5.dr_ref
  116.5 70.3 %grad_sum.1 = (f32[2048,512]{1,0:T(8,128)}, f32[1024,128]{1,0:T(8,128)}) custom-call(f32[4096,512]{1,0:T(8,128)} %get-tuple-element.26.dc_ref, f32[2,1024,128]{2,1,0:T(8,128)} %pad_maximum_fusion.5.dr_ref), custom_call_target="tpu_custom_call" | custom-call | tf_op jit(solution)/shard_map/grad_sum/pallas_call | solution.py:334
  186.8 1.4 fusion.5
  188.3 0.0 copy-start.3
  188.3 0.1 pad_maximum_fusion.6
  188.4 1.1 copy.50
  189.5 0.0 collective-permute-done.6
  189.5 1.1 maximum_select_fusion.2
  190.6 1.2 copy.51
  191.8 0.0 collective-permute-done.7
  191.8 1.1 maximum_select_fusion.3
  192.9 1.2 copy.52
  194.1 0.0 collective-permute-done.4
  194.1 1.4 maximum_select_fusion.1
  195.4 9.5 %copy.48 = bf16[2048,2,128]{2,1,0:T(2,128)(2,1)} copy(bf16[2048,2,128]{2,0,1:T(8,128)(2,1)S(1)} %maximum_select_fusion.1) | data formatting | bytes 2097152
  204.9 0.0 collective-permute-done.5
  204.9 1.8 copy.47
  206.7 4.6 %maximum_select_fusion = f32[2048,2,192]{2,0,1:T(8,128)} fusion(f32[2048,1,192]{2,0,1:T(8,128)S(1)} %bitcast.34, f32[2048,1,192]{2,0,1:T(8,128)} %get-tuple-element.50, pred[]{:T(512)S(6)} %eq.2), kind=kLoop, calls=%fused_computation.1 | loop fusion | flops 2359296 | bytes 6291457 | tf_op jit(solution)/shard_map/jit(_where)/select_n | solution.py:383
  211.4 5.2 %copy.49 = f32[2048,2,192]{0,2,1:T(8,128)} copy(f32[2048,2,192]{2,0,1:T(8,128)} %maximum_select_fusion) | data formatting | bytes 6291456
  216.6 4.6 %copy.69 = f32[2048,512]{1,0:T(8,128)} copy(f32[2048,512]{1,0:T(8,128)} %get-tuple-element.94) | data formatting | bytes 8388608
  (6 shorter events, 0.1 us)
Async XLA Ops:
  0.6 4.3 %copy-start = (bf16[2048,2,128]{2,1,0:T(2,128)(2,1)S(1)}, bf16[2048,2,128]{2,1,0:T(2,128)(2,1)}, u32[]{:S(2)}) copy-start(bf16[2048,2,128]{2,1,0:T(2,128)(2,1)} %param.9) | copy-start | bytes 3145732
  2.0 10.0 %collective-permute-start.1 = (bf16[2048,64]{1,0:T(8,128)(2,1)S(1)}, bf16[2048,64]{1,0:T(8,128)(2,1)}, u32[]{:S(2)}, u32[]{:S(2)}) collective-permute-start(bf16[2048,64]{1,0:T(8,128)(2,1)S(1)} %copy.37), channel_id=1, source_target_pairs={{0,1},{1,0},{2,3},{3,2},{4,5},{5,4},{6,7},{7,6},{8,9},{9,8},{10,11... | collective-permute-start | bytes 786440 | tf_op jit(solution)/shard_map/ppermute | solution.py:360
  4.5 12.1 %collective-permute-start.2 = (bf16[2048,192]{0,1:T(8,128)(2,1)}, bf16[2048,192]{0,1:T(8,128)(2,1)}, u32[]{:S(2)}, u32[]{:S(2)}) collective-permute-start(bf16[2048,192]{0,1:T(8,128)(2,1)} %get-tuple-element.69), channel_id=1, source_target_pairs={{0,1},{1,0},{2,3},{3,2},{4,5},{5,4},{6,7},{7,6},{8,9},{9,8},{10,11... | collective-permute-start | bytes 2359304 | tf_op jit(solution)/shard_map/ppermute | solution.py:360
  8.0 6.3 %collective-permute-start.3 = (bf16[2048,128]{1,0:T(8,128)(2,1)}, bf16[2048,128]{1,0:T(8,128)(2,1)}, u32[]{:S(2)}, u32[]{:S(2)}) collective-permute-start(bf16[2048,128]{1,0:T(8,128)(2,1)} %bitcast.31), channel_id=1, source_target_pairs={{0,1},{1,0},{2,3},{3,2},{4,5},{5,4},{6,7},{7,6},{8,9},{9,8},{10,11... | collective-permute-start | bytes 1572872 | tf_op jit(solution)/shard_map/ppermute | solution.py:360
  8.0 11.8 %collective-permute-start = (bf16[2048,512]{1,0:T(8,128)(2,1)}, bf16[2048,512]{1,0:T(8,128)(2,1)}, u32[]{:S(2)}, u32[]{:S(2)}) collective-permute-start(bf16[2048,512]{1,0:T(8,128)(2,1)} %param.6), channel_id=1, source_target_pairs={{0,1},{1,0},{2,3},{3,2},{4,5},{5,4},{6,7},{7,6},{8,9},{9,8},{10,11... | collective-permute-start | bytes 6291464 | tf_op jit(solution)/shard_map/ppermute | solution.py:360
  58.4 135.7 %collective-permute-start.4 = (bf16[2048,128]{1,0:T(8,128)(2,1)S(1)}, bf16[2048,128]{1,0:T(8,128)(2,1)}, u32[]{:S(2)}, u32[]{:S(2)}) collective-permute-start(bf16[2048,128]{1,0:T(8,128)(2,1)S(1)} %get-tuple-element.65), channel_id=1, source_target_pairs={{0,1},{1,0},{2,3},{3,2},{4,5},{5,4},{6,7},{7,6},{8,9},{9,8},{10,11... | collective-permute-start | bytes 1572872 | tf_op jit(solution)/shard_map/ppermute | solution.py:360
  106.3 83.2 %collective-permute-start.6 = (f32[512,128]{1,0:T(8,128)}, f32[512,128]{1,0:T(8,128)}, u32[]{:S(2)}, u32[]{:S(2)}) collective-permute-start(f32[512,128]{1,0:T(8,128)} %get-tuple-element.30), channel_id=1, source_target_pairs={{0,1},{1,0},{2,3},{3,2},{4,5},{5,4},{6,7},{7,6},{8,9},{9,8},{10,11... | collective-permute-start | bytes 786440 | tf_op jit(solution)/shard_map/ppermute | solution.py:360
  106.8 84.9 %collective-permute-start.7 = (f32[512,128]{1,0:T(8,128)}, f32[512,128]{1,0:T(8,128)}, u32[]{:S(2)}, u32[]{:S(2)}) collective-permute-start(f32[512,128]{1,0:T(8,128)} %get-tuple-element.31), channel_id=1, source_target_pairs={{0,1},{1,0},{2,3},{3,2},{4,5},{5,4},{6,7},{7,6},{8,9},{9,8},{10,11... | collective-permute-start | bytes 786440 | tf_op jit(solution)/shard_map/ppermute | solution.py:360
  106.9 2.8 %copy-start.1 = (f32[4096,192]{1,0:T(8,128)S(1)}, f32[4096,192]{1,0:T(8,128)}, u32[]{:S(2)}) copy-start(f32[4096,192]{1,0:T(8,128)} %get-tuple-element.25) | copy-start | bytes 9437188
  113.0 91.9 %collective-permute-start.5 = (f32[2048,192]{0,1:T(8,128)}, f32[2048,192]{0,1:T(8,128)}, u32[]{:S(2)}, u32[]{:S(2)}) collective-permute-start(f32[2048,192]{0,1:T(8,128)} %copy.46), channel_id=1, source_target_pairs={{0,1},{1,0},{2,3},{3,2},{4,5},{5,4},{6,7},{7,6},{8,9},{9,8},{10,11... | collective-permute-start | bytes 4718600 | tf_op jit(solution)/shard_map/ppermute | solution.py:360
  188.3 1.2 copy-start.3
  188.4 3.4 %copy-start.2 = (f32[512,128]{1,0:T(8,128)S(1)}, f32[512,128]{1,0:T(8,128)}, u32[]{:S(2)}) copy-start(f32[512,128]{1,0:T(8,128)} %get-tuple-element.31) | copy-start | bytes 786436

commit v2 on v0

v2 whole, which is shorter than its diff:
```python
import functools
import math
import jax
import jax.numpy as jnp
from jax import lax
from jax.experimental import pallas as pl
from jax.experimental.pallas import tpu as pltpu
from jax.sharding import PartitionSpec as P
BF = jnp.bfloat16
F32 = jnp.float32
NEG_BIG = -1.0e30
LOG2E = math.log2(math.e)
LANES = 128
BLK = 512
MESH = pl.DeviceIdType.MESH


def mm(a, b):
    return lax.dot_general(a, b, (((1,), (0,)), ((), ())), preferred_element_type=F32)


def mm_nt(a, b):
    return lax.dot_general(a, b, (((1,), (1,)), ((), ())), preferred_element_type=F32)


def mm_tn(a, b):
    return lax.dot_general(a, b, (((0,), (0,)), ((), ())), preferred_element_type=F32)


def kernel(side, c_in, rt_in, qt_in, do_in, wuk_in, wuv_in,
           o_out, dqt_out, dc_out, drt_out, dwk_out, dwv_out,
           c_scr, rt_scr, qt_scr, dor_scr, wk_scr, wv_scr,
           do_scr, kc_scr, v_scr, kt_scr, vt_scr, o_scr, lse_scr, dd_scr,
           m_scr, l_scr, acc_scr, dqt_scr, dk_scr, dv_scr,
           dcp, drp, dro, dwk_scr, dwv_scr, o_far, dwk_far, dwv_far, d2d,
           ra1, ra2, rb1, rb2, rc1, rc2,
           in_loc, in_snd, in_rcv, x_snd, x_rcv, out_loc, out_snd, out_rcv):
    tp = lax.axis_index("tp")
    me = lax.axis_index("cp")
    strides = (1, side, side * side)
    coord = [lax.rem(tp // st, side) for st in strides]
    nbr = [[tp + (lax.rem(coord[a] + off, side) - coord[a]) * strides[a] for off in (1, side - 1)] for a in range(3)]
    mate = {"cp": 1 - me}
    t_all, rank = c_scr.shape
    piece = t_all // 4
    nb = t_all // BLK
    per = piece // BLK
    qk = qt_scr.shape[0]
    dn = wk_scr.shape[1]
    dr = rt_scr.shape[0]
    scale = qk ** -0.5
    scale2 = scale * LOG2E
    cols = rank // LANES
    n_units = 2 * cols + 1

    def mul(x, n):
        return pl.multiple_of(x, n)

    barrier = pltpu.get_barrier_semaphore()
    for a in range(3):
        for b in range(2):
            pl.semaphore_signal(barrier, inc=1, device_id={"tp": nbr[a][b]}, device_id_type=MESH)
    pl.semaphore_signal(barrier, inc=1, device_id=mate, device_id_type=MESH)
    pl.semaphore_wait(barrier, 7)

    def own_piece(w):
        return jnp.where(w == 0, me, 3 - me) if not isinstance(w, int) else (me if w == 0 else 3 - me)

    def in_refs(w, g, head):
        src = pl.ds(mul(w * piece, piece), piece)
        dst = pl.ds(mul(g * piece, piece), piece)
        return [(c_in.at[src, :], c_scr.at[dst, :]), (rt_in.at[:, src], rt_scr.at[:, dst]),
                (qt_in.at[head, :, src], qt_scr.at[:, dst]), (do_in.at[src], dor_scr.at[dst])]

    def in_local(w, g, k):
        s, d = in_refs(w, g, me)[k]
        return pltpu.make_async_copy(s, d, in_loc.at[k, w])

    def in_remote(w, g, k):
        s, d = in_refs(w, g, 1 - me)[k]
        return pltpu.make_async_remote_copy(src_ref=s, dst_ref=d, send_sem=in_snd.at[k, w], recv_sem=in_rcv.at[k, w],
                                            device_id=mate, device_id_type=MESH)

    for w in range(2):
        for k in range(4):
            in_local(w, own_piece(w), k).start()
            in_remote(w, own_piece(w), k).start()

    wk_scr[...] = jnp.where(me == 0, wuk_in[:, 0, :], wuk_in[:, 1, :])
    wv_scr[...] = jnp.where(me == 0, wuv_in[:, 0, :], wuv_in[:, 1, :])

    kpos = lax.broadcasted_iota(jnp.int32, (BLK, BLK), 0)
    qpos = lax.broadcasted_iota(jnp.int32, (BLK, BLK), 1)

    def blk(i):
        return pl.ds(mul(i * BLK, BLK), BLK)

    def fwd_pair(i, j, masked, first):
        s = mm(kc_scr[blk(j), :], qt_scr[:, blk(i)])
        if masked:
            s = jnp.where(kpos <= qpos, s, NEG_BIG)
        m_blk = jnp.max(s, axis=0, keepdims=True)
        m_new = m_blk if first else jnp.maximum(m_scr[...], m_blk)
        e = jnp.exp2(s * scale2 - m_new * scale2)
        l_blk = jnp.sum(e, axis=0, keepdims=True)
        o_blk = mm(vt_scr[j], e.astype(BF))
        if first:
            l_scr[...] = l_blk
            acc_scr[...] = o_blk
        else:
            alpha = jnp.exp2((m_scr[...] - m_new) * scale2)
            l_scr[...] = l_scr[...] * alpha + l_blk
            acc_scr[...] = acc_scr[...] * alpha + o_blk
        m_scr[...] = m_new

    def fwd_block(i, carry):
        g = i // per
        w = g // 2
        mine = (g == me) | (g == 3 - me)

        @pl.when((lax.rem(i, per) == 0) & mine)
        def _():
            for k in range(4):
                in_local(w, g, k).wait()

        @pl.when((lax.rem(i, per) == 0) & jnp.logical_not(mine))
        def _():
            for k in range(4):
                in_remote(w, g, k).wait_recv()

        rows = blk(i)
        cb = c_scr[rows, :]
        kb = mm(cb, wk_scr[...])
        vb = mm(cb, wv_scr[...])
        rtb = rt_scr[:, rows]
        kc_scr[rows, :dn] = kb.astype(BF)
        kc_scr[rows, dn:] = rtb.astype(F32).T.astype(BF)
        kt_scr[i, :dn, :] = kb.T.astype(BF)
        kt_scr[i, dn:, :] = rtb
        v_scr[rows, :] = vb.astype(BF)
        vt_scr[i] = vb.T.astype(BF)
        x = dor_scr[rows]
        do = jnp.where(me == 0, x[:, 0, :], x[:, 1, :])
        do_scr[rows, :] = do
        fwd_pair(i, i, True, True)

        def body(j, cc):
            fwd_pair(i, j, False, False)
            return cc

        lax.fori_loop(0, i, body, 0)
        ot = acc_scr[...] / l_scr[...]
        o_scr[rows, :] = ot.T.astype(BF)
        dd_scr[:, rows] = jnp.sum(do.astype(F32).T * ot, axis=0, keepdims=True)
        lse_scr[:, rows] = m_scr[...] * scale2 + jnp.log2(l_scr[...])
        return carry

    lax.fori_loop(0, nb, fwd_block, 0)

    def rows_of(u, owner, start, n):
        if u == n_units - 1:
            return drp.at[owner, pl.ds(start, n), :]
        w, b = divmod(u, cols)
        g = owner if w == 0 else 3 - owner
        return dcp.at[pl.ds(mul(g * piece + start, 8), n), pl.ds(b * LANES, LANES)]

    def out_at(u, start, n):
        if u == n_units - 1:
            return dro.at[pl.ds(start, n), :]
        w, b = divmod(u, cols)
        return dc_out.at[pl.ds(mul(w * piece + start, 8), n), pl.ds(b * LANES, LANES)]

    def remote(src, dst, u, k, dev):
        return pltpu.make_async_remote_copy(src_ref=src, dst_ref=dst, send_sem=x_snd.at[u, k], recv_sem=x_rcv.at[u, k],
                                            device_id=dev, device_id_type=MESH)

    rbufs = ((ra1, ra2), (rb1, rb2), (rc1, rc2))

    def make_stages(u):
        axes = [(u + t) % 3 for t in range(3)]
        rows_u = piece
        far = lambda: remote(rows_of(u, 1 - me, 0, rows_u), d2d.at[u], u, 0, mate)
        own = lambda s, n: rows_of(u, me, s, n)
        levels = []
        base, size = 0, rows_u
        for t, a in enumerate(axes):
            n = size // side
            levels.append((base, n, a, t))
            base, size = base + coord[a] * n, n

        def spot(lv, off, extra=0):
            base, n, a, t = lv
            return mul(base + lax.rem(coord[a] + off, side) * n + extra, 8)

        def rs_copies(lv):
            base, n, a, t = lv
            h = n // 2
            fwd, bwd = {"tp": nbr[a][0]}, {"tp": nbr[a][1]}
            r1, r2 = rbufs[t]
            k = 1 + 4 * t
            return [lambda: remote(own(spot(lv, 2), h), r1.at[u, 0], u, k, fwd),
                    lambda: remote(own(spot(lv, 2, h), h), r1.at[u, 1], u, k + 1, bwd),
                    lambda: remote(own(spot(lv, 1), n), r2.at[u, 0], u, k + 2, fwd),
                    lambda: remote(own(spot(lv, side - 1), n), r2.at[u, 1], u, k + 3, bwd)]

        def ag_copies(lv):
            base, n, a, t = lv
            h = n // 2
            fwd, bwd = {"tp": nbr[a][0]}, {"tp": nbr[a][1]}
            k = 13 + 4 * t
            def same(s, m, kk, dev):
                r = out_at(u, s, m)
                return remote(r, r, u, kk, dev)
            return [lambda: same(spot(lv, 0), n, k, fwd), lambda: same(spot(lv, 0), n, k + 1, bwd),
                    lambda: same(spot(lv, side - 1), h, k + 2, fwd), lambda: same(spot(lv, 1, h), h, k + 3, bwd)]

        rs = [rs_copies(lv) for lv in levels]
        ag = [ag_copies(lv) for lv in levels]
        copies = [far] + [c for g in rs for c in g] + [c for g in ag for c in g]
        stages = []

        def s_start():
            far().start()

        def s_near():
            far().wait_recv()
            r = own(0, rows_u)
            r[...] = r[...] + d2d[u]
            rs[0][0]().start()
            rs[0][1]().start()

        stages += [s_start, s_near]
        for t in range(3):
            def s_mid(t=t):
                lv = levels[t]
                h = lv[1] // 2
                r1 = rbufs[t][0]
                rs[t][0]().wait_recv()
                p = own(spot(lv, 1), h)
                p[...] = p[...] + r1[u, 0]
                rs[t][2]().start()
                rs[t][1]().wait_recv()
                p = own(spot(lv, side - 1, h), h)
                p[...] = p[...] + r1[u, 1]
                rs[t][3]().start()

            def s_end(t=t):
                lv = levels[t]
                n = lv[1]
                r2 = rbufs[t][1]
                rs[t][2]().wait_recv()
                rs[t][3]().wait_recv()
                p = own(spot(lv, 0), n)
                total = p[...] + r2[u, 0] + r2[u, 1]
                if t < 2:
                    p[...] = total
                    rs[t + 1][0]().start()
                    rs[t + 1][1]().start()
                else:
                    out_at(u, spot(lv, 0), n)[...] = total
                    ag[2][0]().start()
                    ag[2][1]().start()

            stages += [s_mid, s_end]
        for t in (2, 1, 0):
            def s_fwd(t=t):
                ag[t][0]().wait_recv()
                ag[t][2]().start()
                ag[t][1]().wait_recv()
                ag[t][3]().start()

            def s_got(t=t):
                ag[t][2]().wait_recv()
                ag[t][3]().wait_recv()
                if t > 0:
                    ag[t - 1][0]().start()
                    ag[t - 1][1]().start()

            stages += [s_fwd, s_got]
        return stages, copies

    plans = [make_stages(u) for u in range(n_units)]
    n_stage = len(plans[0][0])
    early = list(range(cols, 2 * cols))
    late = list(range(0, cols)) + [n_units - 1]

    def run_stage(k, units):
        for u in units:
            plans[u][0][k]()

    hooks = [11, 12, 14, 16, 18, 20, 22, 24, 26, 29, 30, 32, 34]

    def bwd_block(step, carry):
        j = nb - 1 - step
        t0 = step * (step + 1) // 2
        bwd_diag(j)

        def body(i, cc):
            t = t0 + (i - j)
            for k, tk in enumerate(hooks):
                @pl.when(t == tk)
                def _(k=k):
                    run_stage(k, early)
            bwd_off(j, i)
            return cc

        lax.fori_loop(j + 1, nb, body, 0)
        rows = blk(j)
        dk = dk_scr[...] * scale
        dkb = dk[:, :dn].astype(BF)
        dvb = dv_scr[...].astype(BF)
        dcp[rows, :] = mm_nt(dkb, wk_scr[...]) + mm_nt(dvb, wv_scr[...])
        drt = dk[:, dn:].T
        g = j // per
        owner = jnp.where((g == 0) | (g == 3), 0, 1)
        lt0 = (g // 2) * (piece // LANES) + lax.rem(j, per) * (BLK // LANES)
        for rt in range(dr // 8):
            for lt in range(BLK // LANES):
                row = mul((rt * (2 * piece // LANES) + lt0 + lt) * 8, 8)
                drp[owner, pl.ds(row, 8), :] = drt[rt * 8:rt * 8 + 8, lt * LANES:(lt + 1) * LANES]
        dwk = mm_tn(c_scr[rows, :], dkb)
        dwv = mm_tn(c_scr[rows, :], dvb)

        @pl.when(step == 0)
        def _():
            dwk_scr[...] = dwk
            dwv_scr[...] = dwv

        @pl.when(step > 0)
        def _():
            dwk_scr[...] += dwk
            dwv_scr[...] += dwv

        return carry

    def bwd_core(j, i, masked, first):
        q = qt_scr[:, blk(i)]
        do = do_scr[blk(i), :]
        s = mm(kc_scr[blk(j), :], q)
        p = jnp.exp2(s * scale2 - lse_scr[:, blk(i)])
        if masked:
            p = jnp.where(kpos <= qpos, p, 0.0)
        dp = mm_nt(v_scr[blk(j), :], do)
        ds = (p * (dp - dd_scr[:, blk(i)])).astype(BF)
        dq_blk = mm(kt_scr[j], ds)
        dk_blk = mm_nt(ds, q)
        dv_blk = mm(p.astype(BF), do)
        if first:
            dk_scr[...] = dk_blk
            dv_scr[...] = dv_blk
            dqt_scr[i] = dq_blk
        else:
            dk_scr[...] += dk_blk
            dv_scr[...] += dv_blk
            dqt_scr[i] += dq_blk

    def bwd_diag(j):
        bwd_core(j, j, True, True)

    def bwd_off(j, i):
        bwd_core(j, i, False, False)

    lax.fori_loop(0, nb, bwd_block, 0)

    run_stage(0, late)
    run_stage(n_stage - 1, early)

    def x_o(w):
        g = own_piece(w)
        far_g = (1 - me) if w == 0 else 2 + me
        return pltpu.make_async_remote_copy(src_ref=o_scr.at[pl.ds(mul(far_g * piece, piece), piece), :],
                                            dst_ref=o_far.at[pl.ds(w * piece, piece), :],
                                            send_sem=out_snd.at[w], recv_sem=out_rcv.at[w],
                                            device_id=mate, device_id_type=MESH)

    def x_w(k):
        s, d = ((dwk_scr, dwk_far), (dwv_scr, dwv_far))[k]
        return pltpu.make_async_remote_copy(src_ref=s, dst_ref=d, send_sem=out_snd.at[2 + k], recv_sem=out_rcv.at[2 + k],
                                            device_id=mate, device_id_type=MESH)

    def x_q(w, b):
        far_g = (1 - me) if w == 0 else 2 + me
        return pltpu.make_async_remote_copy(src_ref=dqt_scr.at[far_g * per + b],
                                            dst_ref=dqt_out.at[me, :, pl.ds((w * per + b) * BLK, BLK)],
                                            send_sem=out_snd.at[4 + w * per + b], recv_sem=out_rcv.at[4 + w * per + b],
                                            device_id=mate, device_id_type=MESH)

    for w in range(2):
        x_o(w).start()
    for k in range(2):
        x_w(k).start()
    for i in range(nb):
        dqt_scr[i] = dqt_scr[i] * scale
    for w in range(2):
        for b in range(per):
            x_q(w, b).start()
    run_stage(1, late)
    for w in range(2):
        for b in range(per):
            dqt_out[me, :, pl.ds((w * per + b) * BLK, BLK)] = dqt_scr[own_piece(w) * per + b]
    run_stage(2, late)
    for w in range(2):
        x_o(w).wait_recv()
        mine = o_scr[pl.ds(mul(own_piece(w) * piece, piece), piece), :]
        other = o_far[pl.ds(w * piece, piece), :]
        o_out[pl.ds(w * piece, piece), 0, :] = jnp.where(me == 0, mine, other)
        o_out[pl.ds(w * piece, piece), 1, :] = jnp.where(me == 0, other, mine)
    run_stage(3, late)
    for k, (s, f, o) in enumerate(((dwk_scr, dwk_far, dwk_out), (dwv_scr, dwv_far, dwv_out))):
        x_w(k).wait_recv()
        o[:, 0, :] = jnp.where(me == 0, s[...], f[...])
        o[:, 1, :] = jnp.where(me == 0, f[...], s[...])
    for k in range(4, n_stage):
        run_stage(k, late)
    for rt in range(dr // 8):
        for lt in range(2 * piece // LANES):
            row = (rt * (2 * piece // LANES) + lt) * 8
            drt_out[rt * 8:rt * 8 + 8, lt * LANES:(lt + 1) * LANES] = dro[row:row + 8, :]
    for w in range(2):
        for b in range(per):
            x_q(w, b).wait()
        x_o(w).wait_send()
        x_w(w).wait_send()
        for k in range(4):
            in_remote(w, own_piece(w), k).wait_send()
    for u in range(n_units):
        for cpy in plans[u][1]:
            cpy().wait_send()


def run(c, rt, qt, do, wuk, wuv, side, vmem=60 * 2**20):
    half, rank = c.shape
    t = 2 * half
    dr = rt.shape[0]
    qk = qt.shape[1]
    dn = wuk.shape[2]
    dv = wuv.shape[2]
    nb = t // BLK
    piece = t // 4
    nu = 2 * (rank // LANES) + 1
    sds = jax.ShapeDtypeStruct
    vm = pltpu.VMEM
    bufs = []
    size = piece
    for _ in range(3):
        n = size // side
        bufs += [vm((nu, 2, n // 2, LANES), F32), vm((nu, 2, n, LANES), F32)]
        size = n
    dma = pltpu.SemaphoreType.DMA
    any_spec = pl.BlockSpec(memory_space=pl.ANY)
    vm_spec = pl.BlockSpec(memory_space=pltpu.VMEM)
    return pl.pallas_call(
        functools.partial(kernel, side),
        in_specs=[any_spec] * 4 + [vm_spec] * 2,
        out_specs=[vm_spec] * 6,
        out_shape=[sds((half, 2, dv), BF), sds((2, qk, half), F32), sds((half, rank), F32), sds((dr, half), F32),
                   sds((rank, 2, dn), F32), sds((rank, 2, dv), F32)],
        scratch_shapes=[vm((t, rank), BF), vm((dr, t), BF), vm((qk, t), BF), vm((t, 2, dv), BF), vm((rank, dn), BF), vm((rank, dv), BF),
                        vm((t, dv), BF), vm((t, qk), BF), vm((t, dv), BF), vm((nb, qk, BLK), BF), vm((nb, dv, BLK), BF),
                        vm((t, dv), BF), vm((1, t), F32), vm((1, t), F32),
                        vm((1, BLK), F32), vm((1, BLK), F32), vm((dv, BLK), F32), vm((nb, qk, BLK), F32),
                        vm((BLK, qk), F32), vm((BLK, dv), F32),
                        vm((t, rank), F32), vm((2, piece, LANES), F32), vm((piece, LANES), F32), vm((rank, dn), F32), vm((rank, dv), F32),
                        vm((half, dv), BF), vm((rank, dn), F32), vm((rank, dv), F32), vm((nu, piece, LANES), F32)]
        + bufs + [dma((4, 2)), dma((4, 2)), dma((4, 2)), dma((nu, 25)), dma((nu, 25)), dma((1,)), dma((8,)), dma((8,))],
        compiler_params=pltpu.CompilerParams(collective_id=0, has_side_effects=True, vmem_limit_bytes=vmem),
        name="mla_step",
    )(c, rt, qt, do, wuk, wuv)


def solution(mesh):
    side = round(mesh.shape['tp'] ** (1 / 3))
    seq_spec = P(('dp', 'cp'), None)
    head_spec = P(('dp', 'cp'), 'tp', None)
    weight_spec = P(None, 'tp', None)
    grad_spec = P('dp', 'tp', None)

    def device_fn(c_latent, k_rope, q_heads, d_out, w_uk, w_uv):
        o, dqt, dc, drt, dwk, dwv = run(c_latent, k_rope.T, jnp.transpose(q_heads, (1, 2, 0)), d_out, w_uk, w_uv, side)
        return o, jnp.transpose(dqt, (2, 0, 1)), dc, drt.T, dwk, dwv

    return jax.shard_map(device_fn, mesh=mesh,
                         in_specs=(seq_spec, seq_spec, head_spec, head_spec, weight_spec, weight_spec),
                         out_specs=(head_spec, head_spec, seq_spec, seq_spec, grad_spec, grad_spec),
                         check_vma=False)
```

time: 515 us -> 179 us (0.35)
  the two profiles are of different devices: /device:TPU:1 before, /device:TPU:8 now
where the time goes in v2:
time: 179 us
  Pallas kernels  167 us (93%)
  local copies, waits for them, and re-layouts  11 us (6%)
    pallas_call x1, Pallas kernels, run(): pl.pallas_call(functools.partial(kernel, side), in_specs=[any_spec] * 4 +...  167 us
    unnamed x14, local copies, waits for them, and re-layouts  11 us

profile of v2, /device:TPU:8, one launch (start us, length us, event | category | flops | bytes accessed | tf_op | source)
XLA Modules:
  0.0 179.0 jit_solution(12156035481693113995)
XLA Ops:
  0.6 167.3 %mla_step.1 = (bf16[2048,2,128]{2,1,0:T(2,128)(2,1)}, f32[2,192,2048]{2,1,0:T(8,128)}, f32[2048,512]{1,0:T(8,128)}, f32[64,2048]{1,0:T(8,128)}, f32[512,2,128]{2,1,0:T(2,128)}, /*index=5*/f32[512,2,128]{2,1,0:T(2,128)}) custom-call(bf16[2048,512]{1,0:T(8,128)(2,1)} %c_in.1, bf16[64,2048]{1,0:T(8,128)(2,1)} %bitcast.7, bf16[2,192,2048]{2,1,0:T(8,128)(2,1)} %bitcast.5, ...), custom_call_target="tpu_custom_call" | custom-call | tf_op jit(solution)/shard_map/mla_step/pallas_call | solution.py:452
  167.9 2.6 %copy.18 = bf16[2048,2,128]{2,1,0:T(2,128)(2,1)} copy(bf16[2048,2,128]{2,1,0:T(2,128)(2,1)} %get-tuple-element.24) | data formatting | bytes 2097152
  170.5 0.0 copy-start
  170.5 4.1 %copy.19 = f32[2048,2,192]{0,2,1:T(8,128)} copy(f32[2048,2,192]{0,2,1:T(8,128)} %bitcast.4) | data formatting | bytes 6291456
  174.6 0.0 copy-done
  174.6 0.0 copy-start.3
  174.6 0.0 copy-start.2
  174.6 0.0 copy-start.1
  174.6 2.0 %copy.20 = f32[2048,512]{1,0:T(8,128)} copy(f32[2048,512]{1,0:T(8,128)S(1)} %copy-done) | data formatting | bytes 8388608
  176.6 0.0 copy-done.3
  176.6 0.8 copy.21
  177.4 0.0 copy-done.2
  177.4 0.8 copy.22
  178.2 0.0 copy-done.1
  178.2 0.8 copy.23
Async XLA Ops:
  170.5 4.1 %copy-start = (f32[2048,512]{1,0:T(8,128)S(1)}, f32[2048,512]{1,0:T(8,128)}, u32[]{:S(2)}) copy-start(f32[2048,512]{1,0:T(8,128)} %get-tuple-element.26) | copy-start | bytes 12582916
  174.6 2.0 %copy-start.3 = (f32[64,2048]{1,0:T(8,128)S(1)}, f32[64,2048]{1,0:T(8,128)}, u32[]{:S(2)}) copy-start(f32[64,2048]{1,0:T(8,128)} %get-tuple-element.15) | copy-start | bytes 1572868
  174.6 2.8 %copy-start.2 = (f32[512,2,128]{2,1,0:T(2,128)S(1)}, f32[512,2,128]{2,1,0:T(2,128)}, u32[]{:S(2)}) copy-start(f32[512,2,128]{2,1,0:T(2,128)} %get-tuple-element.28) | copy-start | bytes 1572868
  174.6 3.6 %copy-start.1 = (f32[512,2,128]{2,1,0:T(2,128)S(1)}, f32[512,2,128]{2,1,0:T(2,128)}, u32[]{:S(2)}) copy-start(f32[512,2,128]{2,1,0:T(2,128)} %get-tuple-element.29) | copy-start | bytes 1572868

commit v3 on v2

--- a/solution.py
+++ b/solution.py
@@ -32,7 +32,7 @@
            c_scr, rt_scr, qt_scr, dor_scr, wk_scr, wv_scr,
            do_scr, kc_scr, v_scr, kt_scr, vt_scr, o_scr, lse_scr, dd_scr,
            m_scr, l_scr, acc_scr, dqt_scr, dk_scr, dv_scr,
-           dcp, drp, dro, dwk_scr, dwv_scr, o_far, dwk_far, dwv_far, d2d,
+           wide16_scr, wide_scr, dcp, drp, dro, dwk_scr, dwv_scr, o_far, dwk_far, dwv_far, d2d,
            ra1, ra2, rb1, rb2, rc1, rc2,
            in_loc, in_snd, in_rcv, x_snd, x_rcv, out_loc, out_snd, out_rcv):
     tp = lax.axis_index("tp")
@@ -86,8 +86,19 @@
             in_local(w, own_piece(w), k).start()
             in_remote(w, own_piece(w), k).start()
 
-    wk_scr[...] = jnp.where(me == 0, wuk_in[:, 0, :], wuk_in[:, 1, :])
-    wv_scr[...] = jnp.where(me == 0, wuv_in[:, 0, :], wuv_in[:, 1, :])
+    def unpack(x):
+        x = x.reshape(x.shape[0], 2 * x.shape[2])
+        d = x.shape[1] // 2
+        return jnp.where(me == 0, x[:, :d], x[:, d:])
+
+    def pack(buf, mine, other):
+        d = mine.shape[1]
+        buf[:, :d] = jnp.where(me == 0, mine, other)
+        buf[:, d:] = jnp.where(me == 0, other, mine)
+        return buf[...].reshape(buf.shape[0], 2, d)
+
+    wk_scr[...] = unpack(wuk_in[...])
+    wv_scr[...] = unpack(wuv_in[...])
 
     kpos = lax.broadcasted_iota(jnp.int32, (BLK, BLK), 0)
     qpos = lax.broadcasted_iota(jnp.int32, (BLK, BLK), 1)
@@ -139,8 +150,7 @@
         kt_scr[i, dn:, :] = rtb
         v_scr[rows, :] = vb.astype(BF)
         vt_scr[i] = vb.T.astype(BF)
-        x = dor_scr[rows]
-        do = jnp.where(me == 0, x[:, 0, :], x[:, 1, :])
+        do = unpack(dor_scr[rows])
         do_scr[rows, :] = do
         fwd_pair(i, i, True, True)
 
@@ -403,13 +413,11 @@
         x_o(w).wait_recv()
         mine = o_scr[pl.ds(mul(own_piece(w) * piece, piece), piece), :]
         other = o_far[pl.ds(w * piece, piece), :]
-        o_out[pl.ds(w * piece, piece), 0, :] = jnp.where(me == 0, mine, other)
-        o_out[pl.ds(w * piece, piece), 1, :] = jnp.where(me == 0, other, mine)
+        o_out[pl.ds(w * piece, piece)] = pack(wide16_scr, mine, other)
     run_stage(3, late)
     for k, (s, f, o) in enumerate(((dwk_scr, dwk_far, dwk_out), (dwv_scr, dwv_far, dwv_out))):
         x_w(k).wait_recv()
-        o[:, 0, :] = jnp.where(me == 0, s[...], f[...])
-        o[:, 1, :] = jnp.where(me == 0, f[...], s[...])
+        o[...] = pack(wide_scr, s[...], f[...])
     for k in range(4, n_stage):
         run_stage(k, late)
     for rt in range(dr // 8):
@@ -428,7 +436,7 @@
             cpy().wait_send()
 
 
-def run(c, rt, qt, do, wuk, wuv, side, vmem=60 * 2**20):
+def run(c, rt, qt, do, wuk, wuv, side, vmem=52 * 2**20):
     half, rank = c.shape
     t = 2 * half
     dr = rt.shape[0]
@@ -453,13 +461,13 @@
         functools.partial(kernel, side),
         in_specs=[any_spec] * 4 + [vm_spec] * 2,
         out_specs=[vm_spec] * 6,
-        out_shape=[sds((half, 2, dv), BF), sds((2, qk, half), F32), sds((half, rank), F32), sds((dr, half), F32),
-                   sds((rank, 2, dn), F32), sds((rank, 2, dv), F32)],
+        out_shape=[vm((half, 2, dv), BF), vm((2, qk, half), F32), vm((half, rank), F32), vm((dr, half), F32),
+                   vm((rank, 2, dn), F32), vm((rank, 2, dv), F32)],
         scratch_shapes=[vm((t, rank), BF), vm((dr, t), BF), vm((qk, t), BF), vm((t, 2, dv), BF), vm((rank, dn), BF), vm((rank, dv), BF),
                         vm((t, dv), BF), vm((t, qk), BF), vm((t, dv), BF), vm((nb, qk, BLK), BF), vm((nb, dv, BLK), BF),
                         vm((t, dv), BF), vm((1, t), F32), vm((1, t), F32),
                         vm((1, BLK), F32), vm((1, BLK), F32), vm((dv, BLK), F32), vm((nb, qk, BLK), F32),
-                        vm((BLK, qk), F32), vm((BLK, dv), F32),
+                        vm((BLK, qk), F32), vm((BLK, dv), F32), vm((piece, 2 * dv), BF), vm((rank, 2 * dn), F32),
                         vm((t, rank), F32), vm((2, piece, LANES), F32), vm((piece, LANES), F32), vm((rank, dn), F32), vm((rank, dv), F32),
                         vm((half, dv), BF), vm((rank, dn), F32), vm((rank, dv), F32), vm((nu, piece, LANES), F32)]
         + bufs + [dma((4, 2)), dma((4, 2)), dma((4, 2)), dma((nu, 25)), dma((nu, 25)), dma((1,)), dma((8,)), dma((8,))],

time: 179 us -> 164 us (0.916)
  Pallas kernels: 167 us -> 157 us
  local copies, waits for them, and re-layouts: 11 us -> 7.03 us
    pallas_call x1, Pallas kernels: 167 us -> 157 us  [run(): pl.pallas_call(functools.partial(kernel, side), in_specs=[any_spec] * 4 +...]
    unnamed x14 -> x6, local copies, waits for them, and re-layouts: 11 us -> 7.03 us
where the time goes in v3:
time: 164 us
  Pallas kernels  157 us (96%)
  local copies, waits for them, and re-layouts  7.03 us (4%)
    pallas_call x1, Pallas kernels, run(): pl.pallas_call(functools.partial(kernel, side), in_specs=[any_spec] * 4 +...  157 us
    unnamed x6, local copies, waits for them, and re-layouts  7.03 us

profile of v3, /device:TPU:8, one launch (start us, length us, event | category | flops | bytes accessed | tf_op | source)
XLA Modules:
  0.0 164.3 jit_solution(90419397140755779)
XLA Ops:
  0.6 156.6 %mla_step.1 = (bf16[2048,2,128]{2,1,0:T(2,128)(2,1)S(1)}, f32[2,192,2048]{2,1,0:T(8,128)S(1)}, f32[2048,512]{1,0:T(8,128)S(1)}, f32[64,2048]{1,0:T(8,128)S(1)}, ...) custom-call(bf16[2048,512]{1,0:T(8,128)(2,1)} %c_in.1, bf16[64,2048]{1,0:T(8,128)(2,1)} %bitcast.7, ...), custom_call_target="tpu_custom_call" | custom-call | tf_op jit(solution)/shard_map/mla_step/pallas_call | solution.py:460
  157.3 1.0 copy.18
  158.2 1.7 %copy.19 = f32[2048,2,192]{0,2,1:T(8,128)} copy(f32[2048,2,192]{0,2,1:T(8,128)S(1)} %bitcast.4) | data formatting | bytes 6291456
  159.9 0.8 copy.21
  160.7 0.8 copy.22
  161.5 0.8 copy.23
  162.3 2.0 %copy.20 = f32[2048,512]{1,0:T(8,128)} copy(f32[2048,512]{1,0:T(8,128)S(1)} %get-tuple-element.20) | data formatting | bytes 8388608

commit v4 on v3

v4 whole, which is shorter than its diff:
```python
import functools
import math
import jax
import jax.numpy as jnp
from jax import lax
from jax.experimental import pallas as pl
from jax.experimental.pallas import tpu as pltpu
from jax.sharding import PartitionSpec as P
BF = jnp.bfloat16
F32 = jnp.float32
NEG_BIG = -1.0e30
LOG2E = math.log2(math.e)
LANES = 128
BLK = 512
HOOKS_A = (0, 3, 6, 9, 10, 12, 13)
HOOKS_B = (7, 8, 10, 12, 13)
MESH = pl.DeviceIdType.MESH


def mm(a, b):
    return lax.dot_general(a, b, (((1,), (0,)), ((), ())), preferred_element_type=F32)


def mm_nt(a, b):
    return lax.dot_general(a, b, (((1,), (1,)), ((), ())), preferred_element_type=F32)


def mm_tn(a, b):
    return lax.dot_general(a, b, (((0,), (0,)), ((), ())), preferred_element_type=F32)


def kernel(side, c_in, rt_in, qt_in, do_in, wuk_in, wuv_in,
           o_out, dqt_out, sum_out, drt_out, dwk_out, dwv_out,
           c_scr, rt_scr, qt_scr, dor_scr, wk_scr, wv_scr,
           do_scr, kc_scr, v_scr, kt_scr, vt_scr, o_scr, lse_scr, dd_scr,
           m_scr, l_scr, acc_scr, dqt_scr, dk_scr, dv_scr,
           dkv_scr, wide_scr, dcp, dwk_scr, dwv_scr, o_far, dwk_far, dwv_far, d2d,
           ra1, ra2, rb1, rb2, rc1, rc2,
           in_loc, in_snd, in_rcv, x_snd, x_rcv, out_loc, out_snd, out_rcv):
    tp = lax.axis_index("tp")
    me = lax.axis_index("cp")
    strides = (1, side, side * side)
    coord = [lax.rem(tp // st, side) for st in strides]
    nbr = [[tp + (lax.rem(coord[a] + off, side) - coord[a]) * strides[a] for off in (1, side - 1)] for a in range(3)]
    mate = {"cp": 1 - me}
    t_all, rank = c_scr.shape
    piece = t_all // 4
    nb = t_all // BLK
    per = piece // BLK
    qk = qt_scr.shape[0]
    dn = wk_scr.shape[1]
    dr = rt_scr.shape[0]
    scale = qk ** -0.5
    scale2 = scale * LOG2E
    cols = rank // LANES

    def mul(x, n):
        return pl.multiple_of(x, n)

    barrier = pltpu.get_barrier_semaphore()
    for a in range(3):
        for b in range(2):
            pl.semaphore_signal(barrier, inc=1, device_id={"tp": nbr[a][b]}, device_id_type=MESH)
    pl.semaphore_signal(barrier, inc=1, device_id=mate, device_id_type=MESH)
    pl.semaphore_wait(barrier, 7)

    def own_piece(w):
        return jnp.where(w == 0, me, 3 - me) if not isinstance(w, int) else (me if w == 0 else 3 - me)

    def in_refs(w, g, head):
        src = pl.ds(mul(w * piece, piece), piece)
        dst = pl.ds(mul(g * piece, piece), piece)
        return [(c_in.at[src, :], c_scr.at[dst, :]), (rt_in.at[:, src], rt_scr.at[:, dst]),
                (qt_in.at[head, :, src], qt_scr.at[:, dst]), (do_in.at[src], dor_scr.at[dst])]

    def in_local(w, g, k):
        s, d = in_refs(w, g, me)[k]
        return pltpu.make_async_copy(s, d, in_loc.at[k, w])

    def in_remote(w, g, k):
        s, d = in_refs(w, g, 1 - me)[k]
        return pltpu.make_async_remote_copy(src_ref=s, dst_ref=d, send_sem=in_snd.at[k, w], recv_sem=in_rcv.at[k, w],
                                            device_id=mate, device_id_type=MESH)

    for w in range(2):
        for k in range(4):
            in_local(w, own_piece(w), k).start()
            in_remote(w, own_piece(w), k).start()

    def unpack(x):
        x = x.reshape(x.shape[0], 2 * x.shape[2])
        d = x.shape[1] // 2
        return jnp.where(me == 0, x[:, :d], x[:, d:])

    def pack(buf, mine, other):
        d = mine.shape[1]
        buf[:, :d] = jnp.where(me == 0, mine, other)
        buf[:, d:] = jnp.where(me == 0, other, mine)
        return buf[...].reshape(buf.shape[0], 2, d)

    wk_scr[...] = unpack(wuk_in[...])
    wv_scr[...] = unpack(wuv_in[...])

    def blk(i):
        return pl.ds(mul(i * BLK, BLK), BLK)

    def lo(n):
        return pl.ds(0, n)

    def soft_update(s, vt, cols, first):
        m_blk = jnp.max(s, axis=0, keepdims=True)
        m_new = m_blk if first else jnp.maximum(m_scr[:, cols], m_blk)
        e = jnp.exp2(s * scale2 - m_new * scale2)
        l_blk = jnp.sum(e, axis=0, keepdims=True)
        o_blk = mm(vt, e.astype(BF))
        if first:
            l_scr[:, cols] = l_blk
            acc_scr[:, cols] = o_blk
        else:
            alpha = jnp.exp2((m_scr[:, cols] - m_new) * scale2)
            l_scr[:, cols] = l_scr[:, cols] * alpha + l_blk
            acc_scr[:, cols] = acc_scr[:, cols] * alpha + o_blk
        m_scr[:, cols] = m_new

    def cut(n_k, n_q):
        kp = lax.broadcasted_iota(jnp.int32, (n_k, n_q), 0)
        qp = lax.broadcasted_iota(jnp.int32, (n_k, n_q), 1)
        return kp <= qp

    def fwd_piece(g, carry):
        w = g // 2
        mine = (g == me) | (g == 3 - me)

        @pl.when(mine)
        def _():
            for k in range(4):
                in_local(w, g, k).wait()

        @pl.when(jnp.logical_not(mine))
        def _():
            for k in range(4):
                in_remote(w, g, k).wait_recv()

        rows = pl.ds(mul(g * piece, piece), piece)
        cb = c_scr[rows, :]
        kb = mm(cb, wk_scr[...])
        vb = mm(cb, wv_scr[...])
        rtb = rt_scr[:, rows]
        kc_scr[rows, :dn] = kb.astype(BF)
        kc_scr[rows, dn:] = rtb.astype(F32).T.astype(BF)
        kt_scr[g, :dn, :] = kb.T.astype(BF)
        kt_scr[g, dn:, :] = rtb
        v_scr[rows, :] = vb.astype(BF)
        vt_scr[g] = vb.T.astype(BF)
        do = unpack(dor_scr[rows])
        do_scr[rows, :] = do
        qt = qt_scr[:, rows]
        low = pl.ds(mul(g * piece, piece), BLK)
        high = pl.ds(mul(g * piece + BLK, BLK), BLK)
        s = mm(kc_scr[low, :], qt)
        soft_update(jnp.where(cut(BLK, piece), s, NEG_BIG), vt_scr[g, :, :BLK], slice(None), True)
        s = mm(kc_scr[high, :], qt_scr[:, high])
        soft_update(jnp.where(cut(BLK, BLK), s, NEG_BIG), vt_scr[g, :, BLK:], slice(BLK, piece), False)

        def body(j, cc):
            fwd_full(g, j)
            return cc

        lax.fori_loop(0, g, body, 0)
        ot = acc_scr[...] / l_scr[...]
        o_scr[rows, :] = ot.T.astype(BF)
        dd_scr[:, rows] = jnp.sum(do.astype(F32).T * ot, axis=0, keepdims=True)
        lse_scr[:, rows] = m_scr[...] * scale2 + jnp.log2(l_scr[...])
        return carry

    ra, rb, cs = 128, 256, BLK

    def fwd_full(g, j):
        mx, st = {}, {}
        bufs = (dcp.at[:piece, :], dcp.at[piece:2 * piece, :])

        def score(c, r):
            s = mm(kc_scr[pl.ds(mul(j * piece + r * ra, ra), ra), :], qt_scr[:, pl.ds(mul(g * piece + c * cs, cs), cs)])
            bufs[c % 2][r * ra:(r + 1) * ra, :] = s
            p = jnp.max(s, axis=0, keepdims=True)
            mx[c] = p if c not in mx else jnp.maximum(mx[c], p)

        def mid(c):
            cols = slice(c * cs, (c + 1) * cs)
            m_old = m_scr[:, cols]
            m_new = jnp.maximum(m_old, mx[c])
            m_scr[:, cols] = m_new
            st[c] = [m_new * scale2, jnp.exp2((m_old - m_new) * scale2), None, None]

        def weigh(c, r):
            d = st[c]
            e = jnp.exp2(bufs[c % 2][r * rb:(r + 1) * rb, :] * scale2 - d[0])
            p = jnp.sum(e, axis=0, keepdims=True)
            o = mm(vt_scr[j, :, r * rb:(r + 1) * rb], e.astype(BF))
            d[2] = p if d[2] is None else d[2] + p
            d[3] = o if d[3] is None else d[3] + o

        def fin(c):
            cols = slice(c * cs, (c + 1) * cs)
            d = st[c]
            l_scr[:, cols] = l_scr[:, cols] * d[1] + d[2]
            acc_scr[:, cols] = acc_scr[:, cols] * d[1] + d[3]

        na, nr = piece // ra, piece // rb
        for r in range(na):
            score(0, r)
        for c in range(piece // cs):
            mid(c)
            for r in range(na):
                if c + 1 < piece // cs:
                    score(c + 1, r)
                if r % (na // nr) == na // nr - 1:
                    weigh(c, r // (na // nr))
            fin(c)

    lax.fori_loop(0, 4, fwd_piece, 0)

    rbufs = ((ra1, ra2), (rb1, rb2), (rc1, rc2))
    sets = {"a": ((2, cols, 0), (3, cols, 1)), "b": ((1, cols, 0),), "c": ((0, cols, 0), (4, 2, 1))}

    def pick(a, xs):
        return jnp.where(a == 0, xs[0], jnp.where(a == 1, xs[1], xs[2]))

    class Unit:
        def __init__(self, wh, b, turn):
            self.wh, self.b = wh, b
            self.u = wh * cols + b
            self.lanes = pl.ds(mul(b * LANES, LANES), LANES)
            first = lax.rem(b + turn, 3)
            self.level = []
            base, size = 0, BLK
            for t in range(3):
                a = lax.rem(first + t, 3)
                n = size // side
                here = pick(a, coord)
                self.level.append((base, n, here, pick(a, [x[0] for x in nbr]), pick(a, [x[1] for x in nbr])))
                base, size = base + here * n, n

        def part(self, owner, start, n):
            if self.wh == 4:
                top = t_all + owner * BLK
            else:
                top = (owner if self.wh < 2 else 3 - owner) * piece + (self.wh % 2) * BLK
            return dcp.at[pl.ds(mul(top + start, 8), n), self.lanes]

        def own(self, start, n):
            return self.part(me, start, n)

        def out(self, start, n):
            return sum_out.at[pl.ds(mul(self.wh * BLK + start, 8), n), self.lanes]

        def spot(self, t, off, extra=0):
            base, n, here, _, _ = self.level[t]
            return base + lax.rem(here + off, side) * n + extra

        def copy(self, src, dst, k, dev):
            return pltpu.make_async_remote_copy(src_ref=src, dst_ref=dst, send_sem=x_snd.at[self.u, k],
                                                recv_sem=x_rcv.at[self.u, k], device_id=dev, device_id_type=MESH)

        def swap(self):
            return self.copy(self.part(1 - me, 0, BLK), d2d.at[self.u], 0, mate)

        def half(self, t):
            n = self.level[t][1]
            return (n // 2, True) if n % 16 == 0 else (n, False)

        def rs(self, t, q):
            _, n, _, fwd, bwd = self.level[t]
            h, _ = self.half(t)
            r1, r2 = rbufs[t]
            src, dst, dev = ((self.spot(t, 2), r1.at[self.u, 0], fwd), (self.spot(t, 2, h), r1.at[self.u, 1], bwd),
                             (self.spot(t, 1), r2.at[self.u, 0], fwd), (self.spot(t, side - 1), r2.at[self.u, 1], bwd))[q]
            return self.copy(self.own(src, h if q < 2 else n), dst, 1 + 4 * t + q, {"tp": dev})

        def ag(self, t, q):
            _, n, _, fwd, bwd = self.level[t]
            h, _ = self.half(t)
            at, m, dev = ((self.spot(t, 0), n, fwd), (self.spot(t, 0), n, bwd),
                          (self.spot(t, side - 1), h, fwd), (self.spot(t, 1, h), h, bwd))[q]
            r = self.out(at, m)
            return self.copy(r, r, 13 + 4 * t + q, {"tp": dev})

        def all_copies(self):
            res = [self.swap()]
            for t in range(3):
                two = self.half(t)[1]
                res += [self.rs(t, q) for q in range(4) if two or q != 1]
                res += [self.ag(t, q) for q in range(4) if two or q != 3]
            return res

        def start_rs(self, t):
            self.rs(t, 0).start()
            if self.half(t)[1]:
                self.rs(t, 1).start()

        def start_ag(self, t):
            self.ag(t, 0).start()
            self.ag(t, 1).start()

        def stage(self, k):
            if k == 0:
                self.swap().start()
            elif k == 1:
                self.swap().wait_recv()
                r = self.own(0, BLK)
                r[...] = r[...] + d2d[self.u]
                self.start_rs(0)
            elif k < 8:
                t, last = divmod(k - 2, 2)
                n = self.level[t][1]
                h, two = self.half(t)
                r1, r2 = rbufs[t]
                if not last:
                    self.rs(t, 0).wait_recv()
                    p = self.own(self.spot(t, 1), h)
                    p[...] = p[...] + r1[self.u, 0]
                    self.rs(t, 2).start()
                    if two:
                        self.rs(t, 1).wait_recv()
                        p = self.own(self.spot(t, side - 1, h), h)
                        p[...] = p[...] + r1[self.u, 1]
                    self.rs(t, 3).start()
                else:
                    self.rs(t, 2).wait_recv()
                    self.rs(t, 3).wait_recv()
                    p = self.own(self.spot(t, 0), n)
                    total = p[...] + r2[self.u, 0] + r2[self.u, 1]
                    if t < 2:
                        p[...] = total
                        self.start_rs(t + 1)
                    else:
                        self.out(self.spot(t, 0), n)[...] = total
                        self.start_ag(2)
            else:
                t, last = divmod(k - 8, 2)
                t = 2 - t
                two = self.half(t)[1]
                if not last:
                    self.ag(t, 0).wait_recv()
                    self.ag(t, 2).start()
                    self.ag(t, 1).wait_recv()
                    if two:
                        self.ag(t, 3).start()
                else:
                    self.ag(t, 2).wait_recv()
                    if two:
                        self.ag(t, 3).wait_recv()
                    if t > 0:
                        self.start_ag(t - 1)

    n_stage = 14

    def each(name, fn):
        for wh, n, turn in sets[name]:
            def body(b, cc, wh=wh, turn=turn):
                fn(Unit(wh, b, turn))
                return cc
            lax.fori_loop(0, n, body, 0)

    def run_stage(k, name):
        each(name, lambda un: un.stage(k))

    plan_a = dict(zip(HOOKS_A, range(len(HOOKS_A))))
    plan_b = dict(zip(HOOKS_B, range(len(HOOKS_B))))

    def hook(t):
        for at in sorted(set(plan_a) | set(plan_b)):
            @pl.when(t == at)
            def _(at=at):
                if at in plan_a:
                    run_stage(plan_a[at], "a")
                if at in plan_b:
                    run_stage(plan_b[at], "b")

    def bwd_core(j, q_rows, kt, mask, first, dq_at):
        q = qt_scr[:, q_rows]
        do = do_scr[q_rows, :]
        s = mm(kc_scr[blk(j), :], q)
        p = jnp.exp2(s * scale2 - lse_scr[:, q_rows])
        if mask is not None:
            p = jnp.where(mask, p, 0.0)
        dp = mm_nt(v_scr[blk(j), :], do)
        ds = (p * (dp - dd_scr[:, q_rows])).astype(BF)
        dq_at[...] += mm(kt, ds)
        dk_blk = mm_nt(ds, q)
        dv_blk = mm(p.astype(BF), do)
        if first:
            dk_scr[...] = dk_blk
            dv_scr[...] = dv_blk
        else:
            dk_scr[...] += dk_blk
            dv_scr[...] += dv_blk

    def bwd_block(step, carry):
        half = step // 4
        s_ = step - 4 * half
        j = 4 * (1 - half) + 3 - 2 * lax.rem(s_, 2) - s_ // 2
        g = j // per
        odd = lax.rem(j, per)
        t0 = 3 * s_ + s_ // 2 - 1000 * (1 - half)
        off = mul(odd * BLK, BLK)

        def body(i, cc):
            hook(t0 + (i - g))

            @pl.when((i == g) & (odd == 1))
            def _():
                high = pl.ds(mul(g * piece + BLK, BLK), BLK)
                bwd_core(j, high, kt_scr[g, :, BLK:], cut(BLK, BLK), True, dqt_scr.at[g, :, BLK:])

            @pl.when((i == g) & (odd == 0))
            def _():
                bwd_core(j, pl.ds(mul(g * piece, piece), piece), kt_scr[g, :, :BLK], cut(BLK, piece), True, dqt_scr.at[g])

            @pl.when(i > g)
            def _():
                bwd_core(j, pl.ds(mul(i * piece, piece), piece), kt_scr[g, :, pl.ds(off, BLK)], None, False, dqt_scr.at[i])

            return cc

        lax.fori_loop(g, 4, body, 0)
        rows = blk(j)
        dk = dk_scr[...] * scale
        dkb = dk[:, :dn].astype(BF)
        dvb = dv_scr[...].astype(BF)
        dkv_scr[rows, :dn] = dkb
        dkv_scr[rows, dn:] = dvb
        dcp[rows, :] = mm_nt(dkb, wk_scr[...]) + mm_nt(dvb, wv_scr[...])
        drt = dk[:, dn:].T
        owner = jnp.where((g == 0) | (g == 3), 0, 1)
        lt0 = (g // 2) * (piece // LANES) + odd * (BLK // LANES)
        lts = 2 * piece // LANES
        for rt in range(dr // 8):
            b, r = divmod(rt * lts * 8, BLK)
            for lt in range(BLK // LANES):
                row = mul(t_all + owner * BLK + r + (lt0 + lt) * 8, 8)
                dcp[pl.ds(row, 8), b * LANES:(b + 1) * LANES] = drt[rt * 8:rt * 8 + 8, lt * LANES:(lt + 1) * LANES]
        return carry

    def d_weights(lo_j, hi_j):
        def body(j, cc):
            rows = blk(j)
            dwk_scr[...] += mm_tn(c_scr[rows, :], dkv_scr[rows, :dn])
            dwv_scr[...] += mm_tn(c_scr[rows, :], dkv_scr[rows, dn:])
            return cc

        lax.fori_loop(lo_j, hi_j, body, 0)

    def x_o(w):
        g = own_piece(w)
        far_g = (1 - me) if w == 0 else 2 + me
        return pltpu.make_async_remote_copy(src_ref=o_scr.at[pl.ds(mul(far_g * piece, piece), piece), :],
                                            dst_ref=o_far.at[pl.ds(w * piece, piece), :],
                                            send_sem=out_snd.at[w], recv_sem=out_rcv.at[w],
                                            device_id=mate, device_id_type=MESH)

    def x_w(k):
        s, d = ((dwk_scr, dwk_far), (dwv_scr, dwv_far))[k]
        return pltpu.make_async_remote_copy(src_ref=s, dst_ref=d, send_sem=out_snd.at[2 + k], recv_sem=out_rcv.at[2 + k],
                                            device_id=mate, device_id_type=MESH)

    def x_q(w):
        far_g = (1 - me) if w == 0 else 2 + me
        return pltpu.make_async_remote_copy(src_ref=dqt_scr.at[far_g], dst_ref=dqt_out.at[me, :, pl.ds(w * piece, piece)],
                                            send_sem=out_snd.at[4 + w], recv_sem=out_rcv.at[4 + w],
                                            device_id=mate, device_id_type=MESH)

    for w in range(2):
        x_o(w).start()
    for g in range(4):
        dqt_scr[g] = jnp.zeros(dqt_scr.shape[1:], F32)
    dwk_scr[...] = jnp.zeros_like(dwk_scr)
    dwv_scr[...] = jnp.zeros_like(dwv_scr)
    lax.fori_loop(0, nb, bwd_block, 0)

    done_a, done_b = len(HOOKS_A), len(HOOKS_B)

    def tail(k):
        run_stage(k, "c")
        if k + done_b < n_stage:
            run_stage(k + done_b, "b")
        if k + done_a < n_stage:
            run_stage(k + done_a, "a")

    tail(0)
    for g in range(4):
        dqt_scr[g] = dqt_scr[g] * scale
    for w in range(2):
        x_q(w).start()
    tail(1)
    d_weights(0, nb // 2)
    tail(2)
    d_weights(nb // 2, nb)
    for k in range(2):
        x_w(k).start()
    tail(3)
    for w in range(2):
        dqt_out[me, :, pl.ds(w * piece, piece)] = dqt_scr[own_piece(w)]
    tail(4)
    for w in range(2):
        x_o(w).wait_recv()
        mine = o_scr[pl.ds(mul(own_piece(w) * piece, piece), piece), :]
        o_out[pl.ds(w * piece, piece)] = pack(dkv_scr.at[pl.ds(0, piece), :], mine, o_far[pl.ds(w * piece, piece), :])
    tail(5)
    for k, (s_, f_, o_) in enumerate(((dwk_scr, dwk_far, dwk_out), (dwv_scr, dwv_far, dwv_out))):
        x_w(k).wait_recv()
        o_[...] = pack(wide_scr, s_[...], f_[...])
    for k in range(6, n_stage):
        tail(k)
    for rt in range(dr // 8):
        for lt in range(2 * piece // LANES):
            b, r = divmod((rt * (2 * piece // LANES) + lt) * 8, BLK)
            r += 2 * piece
            drt_out[rt * 8:rt * 8 + 8, lt * LANES:(lt + 1) * LANES] = sum_out[r:r + 8, b * LANES:(b + 1) * LANES]
    for w in range(2):
        x_q(w).wait()
        x_o(w).wait_send()
        x_w(w).wait_send()
        for k in range(4):
            in_remote(w, own_piece(w), k).wait_send()

    def drain(un):
        for cpy in un.all_copies():
            cpy.wait_send()

    for name in sets:
        each(name, drain)


def run(c, rt, qt, do, wuk, wuv, side, vmem=51 * 2**20):
    half, rank = c.shape
    t = 2 * half
    dr = rt.shape[0]
    qk = qt.shape[1]
    dn = wuk.shape[2]
    dv = wuv.shape[2]
    nb = t // BLK
    piece = t // 4
    nu = 4 * (rank // LANES) + 2
    sds = jax.ShapeDtypeStruct
    vm = pltpu.VMEM
    bufs = []
    size = BLK
    for _ in range(3):
        n = size // side
        h = n // 2 if n % 16 == 0 else n
        bufs += [vm((nu, 2, h, LANES), F32), vm((nu, 2, n, LANES), F32)]
        size = n
    dma = pltpu.SemaphoreType.DMA
    any_spec = pl.BlockSpec(memory_space=pl.ANY)
    vm_spec = pl.BlockSpec(memory_space=pltpu.VMEM)
    return pl.pallas_call(
        functools.partial(kernel, side),
        in_specs=[any_spec] * 4 + [vm_spec] * 2,
        out_specs=[vm_spec] * 6,
        out_shape=[vm((half, 2, dv), BF), vm((2, qk, half), F32), vm((half + BLK, rank), F32), vm((dr, half), F32),
                   vm((rank, 2, dn), F32), vm((rank, 2, dv), F32)],
        scratch_shapes=[vm((t, rank), BF), vm((dr, t), BF), vm((qk, t), BF), vm((t, 2, dv), BF), vm((rank, dn), BF), vm((rank, dv), BF),
                        vm((t, dv), BF), vm((t, qk), BF), vm((t, dv), BF), vm((4, qk, piece), BF), vm((4, dv, piece), BF),
                        vm((t, dv), BF), vm((1, t), F32), vm((1, t), F32),
                        vm((1, piece), F32), vm((1, piece), F32), vm((dv, piece), F32), vm((4, qk, piece), F32),
                        vm((BLK, qk), F32), vm((BLK, dv), F32), vm((t, dn + dv), BF), vm((rank, 2 * dn), F32),
                        vm((t + 2 * BLK, rank), F32), vm((rank, dn), F32), vm((rank, dv), F32),
                        vm((half, dv), BF), vm((rank, dn), F32), vm((rank, dv), F32), vm((nu, BLK, LANES), F32)]
        + bufs + [dma((4, 2)), dma((4, 2)), dma((4, 2)), dma((nu, 25)), dma((nu, 25)), dma((1,)), dma((8,)), dma((8,))],
        compiler_params=pltpu.CompilerParams(collective_id=0, has_side_effects=True, vmem_limit_bytes=vmem),
        name="mla_step",
    )(c, rt, qt, do, wuk, wuv)


def solution(mesh):
    side = round(mesh.shape['tp'] ** (1 / 3))
    seq_spec = P(('dp', 'cp'), None)
    head_spec = P(('dp', 'cp'), 'tp', None)
    weight_spec = P(None, 'tp', None)
    grad_spec = P('dp', 'tp', None)

    def device_fn(c_latent, k_rope, q_heads, d_out, w_uk, w_uv):
        o, dqt, dc, drt, dwk, dwv = run(c_latent, k_rope.T, jnp.transpose(q_heads, (1, 2, 0)), d_out, w_uk, w_uv, side)
        return o, jnp.transpose(dqt, (2, 0, 1)), dc[:c_latent.shape[0]], drt.T, dwk, dwv

    return jax.shard_map(device_fn, mesh=mesh,
                         in_specs=(seq_spec, seq_spec, head_spec, head_spec, weight_spec, weight_spec),
                         out_specs=(head_spec, head_spec, seq_spec, seq_spec, grad_spec, grad_spec),
                         check_vma=False)
```

time: 164 us -> 138 us (0.84)
  the two profiles are of different devices: /device:TPU:8 before, /device:TPU:0 now
where the time goes in v4:
time: 138 us; the launch traced here: 137 us
  Pallas kernels  129 us (93%)
  local copies, waits for them, and re-layouts  7.47 us (5%)
    pallas_call x1, Pallas kernels, run(): pl.pallas_call(functools.partial(kernel, side), in_specs=[any_spec] * 4 +...  129 us
    unnamed x5, local copies, waits for them, and re-layouts  5.01 us

profile of v4, /device:TPU:0, one launch (start us, length us, event | category | flops | bytes accessed | tf_op | source)
XLA Modules:
  0.0 137.4 jit_solution(6387491313326244586)
XLA Ops:
  0.6 129.3 %mla_step.1 = (bf16[2048,2,128]{2,1,0:T(2,128)(2,1)S(1)}, f32[2,192,2048]{2,1,0:T(8,128)S(1)}, f32[2560,512]{1,0:T(8,128)S(1)}, f32[64,2048]{1,0:T(8,128)S(1)}, ...) custom-call(bf16[2048,512]{1,0:T(8,128)(2,1)} %c_in.1, bf16[64,2048]{1,0:T(8,128)(2,1)} %bitcast.7, ...), custom_call_target="tpu_custom_call" | custom-call | tf_op jit(solution)/shard_map/mla_step/pallas_call | solution.py:557
  129.9 1.0 copy.17
  130.9 1.7 %copy.18 = f32[2048,2,192]{0,2,1:T(8,128)} copy(f32[2048,2,192]{0,2,1:T(8,128)S(1)} %bitcast.4) | data formatting | bytes 6291456
  132.5 0.8 copy.19
  133.3 0.8 copy.20
  134.1 0.8 copy.21
  134.9 2.5 %slice.3 = f32[2048,512]{1,0:T(8,128)} slice(f32[2560,512]{1,0:T(8,128)S(1)} %get-tuple-element.14), slice={[0:2048], [0:512]} | slice | bytes 8388608 | tf_op jit(solution)/shard_map/slice | solution.py:585

commit v5 on v4

--- a/solution.py
+++ b/solution.py
@@ -12,8 +12,10 @@
 LOG2E = math.log2(math.e)
 LANES = 128
 BLK = 512
-HOOKS_A = (0, 3, 6, 9, 10, 12, 13)
-HOOKS_B = (7, 8, 10, 12, 13)
+HOOKS = {2: [(1, "p3", 0)], 5: [(0, "p3", 1)], 8: [(0, "p3", 2)], 10: [(1, "p0", 0)], 11: [(0, "p3", 3)],
+         13: [(0, "p3", 4), (0, "p0", 1)], 14: [(0, "p2", 0)], 15: [(0, "p3", 5)], 16: [(0, "p0", 2)],
+         17: [(0, "p3", 6), (1, "p2", 1), (0, "p1h", 0)], 19: [(0, "p3", 7), (0, "p0", 3), (1, "p2", 2), (1, "p1h", 1)]}
+TAIL = ((0, "p3", 8), (0, "p0", 4), (1, "p2", 3), (1, "p1h", 2), (1, "p1l", 0))
 MESH = pl.DeviceIdType.MESH
 
 
@@ -31,12 +33,12 @@
 
 def kernel(side, c_in, rt_in, qt_in, do_in, wuk_in, wuv_in,
            o_out, dqt_out, sum_out, drt_out, dwk_out, dwv_out,
-           c_scr, rt_scr, qt_scr, dor_scr, wk_scr, wv_scr,
+           c_scr, rt_scr, qt_scr, dor_scr, wkv_scr,
            do_scr, kc_scr, v_scr, kt_scr, vt_scr, o_scr, lse_scr, dd_scr,
            m_scr, l_scr, acc_scr, dqt_scr, dk_scr, dv_scr,
-           dkv_scr, wide_scr, dcp, dwk_scr, dwv_scr, o_far, dwk_far, dwv_far, d2d,
+           dkv_scr, wide_scr, dcp, dw_scr, o_far, dw_far, d2d,
            ra1, ra2, rb1, rb2, rc1, rc2,
-           in_loc, in_snd, in_rcv, x_snd, x_rcv, out_loc, out_snd, out_rcv):
+           in_loc, in_snd, in_rcv, x_snd, x_rcv, out_snd, out_rcv):
     tp = lax.axis_index("tp")
     me = lax.axis_index("cp")
     strides = (1, side, side * side)
@@ -48,7 +50,7 @@
     nb = t_all // BLK
     per = piece // BLK
     qk = qt_scr.shape[0]
-    dn = wk_scr.shape[1]
+    dn = dwk_out.shape[2]
     dr = rt_scr.shape[0]
     scale = qk ** -0.5
     scale2 = scale * LOG2E
@@ -98,8 +100,8 @@
         buf[:, d:] = jnp.where(me == 0, other, mine)
         return buf[...].reshape(buf.shape[0], 2, d)
 
-    wk_scr[...] = unpack(wuk_in[...])
-    wv_scr[...] = unpack(wuv_in[...])
+    wkv_scr[:, :dn] = unpack(wuk_in[...])
+    wkv_scr[:, dn:] = unpack(wuv_in[...])
 
     def blk(i):
         return pl.ds(mul(i * BLK, BLK), BLK)
@@ -143,8 +145,8 @@
 
         rows = pl.ds(mul(g * piece, piece), piece)
         cb = c_scr[rows, :]
-        kb = mm(cb, wk_scr[...])
-        vb = mm(cb, wv_scr[...])
+        kv = mm(cb, wkv_scr[...])
+        kb, vb = kv[:, :dn], kv[:, dn:]
         rtb = rt_scr[:, rows]
         kc_scr[rows, :dn] = kb.astype(BF)
         kc_scr[rows, dn:] = rtb.astype(F32).T.astype(BF)
@@ -221,7 +223,8 @@
     lax.fori_loop(0, 4, fwd_piece, 0)
 
     rbufs = ((ra1, ra2), (rb1, rb2), (rc1, rc2))
-    sets = {"a": ((2, cols, 0), (3, cols, 1)), "b": ((1, cols, 0),), "c": ((0, cols, 0), (4, 2, 1))}
+    sets = {"p3": ((2, cols, 0), (3, cols, 1)), "p0": ((0, cols, 0), (1, cols, 1), (4, 2, 0)),
+            "p2": ((2, cols, 0), (3, cols, 1)), "p1h": ((1, cols, 0),), "p1l": ((0, cols, 0), (4, 2, 1))}
 
     def pick(a, xs):
         return jnp.where(a == 0, xs[0], jnp.where(a == 1, xs[1], xs[2]))
@@ -258,12 +261,12 @@
             base, n, here, _, _ = self.level[t]
             return base + lax.rem(here + off, side) * n + extra
 
-        def copy(self, src, dst, k, dev):
-            return pltpu.make_async_remote_copy(src_ref=src, dst_ref=dst, send_sem=x_snd.at[self.u, k],
+        def copy(self, src, dst, k, dev, slot):
+            return pltpu.make_async_remote_copy(src_ref=src, dst_ref=dst, send_sem=x_snd.at[self.u, slot],
                                                 recv_sem=x_rcv.at[self.u, k], device_id=dev, device_id_type=MESH)
 
         def swap(self):
-            return self.copy(self.part(1 - me, 0, BLK), d2d.at[self.u], 0, mate)
+            return self.copy(self.part(1 - me, 0, BLK), d2d.at[self.u], 0, mate, 2)
 
         def half(self, t):
             n = self.level[t][1]
@@ -275,7 +278,7 @@
             r1, r2 = rbufs[t]
             src, dst, dev = ((self.spot(t, 2), r1.at[self.u, 0], fwd), (self.spot(t, 2, h), r1.at[self.u, 1], bwd),
                              (self.spot(t, 1), r2.at[self.u, 0], fwd), (self.spot(t, side - 1), r2.at[self.u, 1], bwd))[q]
-            return self.copy(self.own(src, h if q < 2 else n), dst, 1 + 4 * t + q, {"tp": dev})
+            return self.copy(self.own(src, h if q < 2 else n), dst, 1 + 4 * t + q, {"tp": dev}, q % 2)
 
         def ag(self, t, q):
             _, n, _, fwd, bwd = self.level[t]
@@ -283,15 +286,19 @@
             at, m, dev = ((self.spot(t, 0), n, fwd), (self.spot(t, 0), n, bwd),
                           (self.spot(t, side - 1), h, fwd), (self.spot(t, 1, h), h, bwd))[q]
             r = self.out(at, m)
-            return self.copy(r, r, 13 + 4 * t + q, {"tp": dev})
-
-        def all_copies(self):
-            res = [self.swap()]
-            for t in range(3):
-                two = self.half(t)[1]
-                res += [self.rs(t, q) for q in range(4) if two or q != 1]
-                res += [self.ag(t, q) for q in range(4) if two or q != 3]
-            return res
+            return self.copy(r, r, 13 + 4 * t + q, {"tp": dev}, q % 2)
+
+        def sent(self, k):
+            if k < 1:
+                return []
+            if k < 7:
+                t, second = divmod(k - 1, 2)
+                qs, f = ((2, 3) if second else (0, 1) if self.half(t)[1] else (0,)), self.rs
+            else:
+                t, second = divmod(k - 7, 2)
+                t = 2 - t
+                qs, f = ((0, 1) if not second else (2, 3) if self.half(t)[1] else (2,)), self.ag
+            return [] if t < 0 else [f(t, q) for q in qs]
 
         def start_rs(self, t):
             self.rs(t, 0).start()
@@ -303,9 +310,9 @@
             self.ag(t, 1).start()
 
         def stage(self, k):
-            if k == 0:
-                self.swap().start()
-            elif k == 1:
+            for cpy in self.sent(k - 1):
+                cpy.wait_send()
+            if k == 1:
                 self.swap().wait_recv()
                 r = self.own(0, BLK)
                 r[...] = r[...] + d2d[self.u]
@@ -365,17 +372,23 @@
     def run_stage(k, name):
         each(name, lambda un: un.stage(k))
 
-    plan_a = dict(zip(HOOKS_A, range(len(HOOKS_A))))
-    plan_b = dict(zip(HOOKS_B, range(len(HOOKS_B))))
+    def run_for(core, items):
+        @pl.when(me == core)
+        def _():
+            for name, k in items:
+                if k == 0:
+                    each(name, lambda un: un.swap().start())
+                else:
+                    run_stage(k, name)
 
     def hook(t):
-        for at in sorted(set(plan_a) | set(plan_b)):
+        for at in sorted(HOOKS):
             @pl.when(t == at)
             def _(at=at):
-                if at in plan_a:
-                    run_stage(plan_a[at], "a")
-                if at in plan_b:
-                    run_stage(plan_b[at], "b")
+                for core in range(2):
+                    items = [(name, k) for c, name, k in HOOKS[at] if c == core]
+                    if items:
+                        run_for(core, items)
 
     def bwd_core(j, q_rows, kt, mask, first, dq_at):
         q = qt_scr[:, q_rows]
@@ -397,12 +410,11 @@
             dv_scr[...] += dv_blk
 
     def bwd_block(step, carry):
-        half = step // 4
-        s_ = step - 4 * half
-        j = 4 * (1 - half) + 3 - 2 * lax.rem(s_, 2) - s_ // 2
-        g = j // per
-        odd = lax.rem(j, per)
-        t0 = 3 * s_ + s_ // 2 - 1000 * (1 - half)
+        pair, low = step // per, lax.rem(step, per)
+        g = jnp.where(pair == 0, 3, jnp.where(pair == 1, 0, jnp.where(pair == 2, 2, 1)))
+        j = g * per + 1 - low
+        odd = 1 - low
+        t0 = jnp.where(pair == 0, low, jnp.where(pair == 1, 2 + 4 * low, jnp.where(pair == 2, 10 + 2 * low, 14 + 3 * low)))
         off = mul(odd * BLK, BLK)
 
         def body(i, cc):
@@ -430,7 +442,7 @@
         dvb = dv_scr[...].astype(BF)
         dkv_scr[rows, :dn] = dkb
         dkv_scr[rows, dn:] = dvb
-        dcp[rows, :] = mm_nt(dkb, wk_scr[...]) + mm_nt(dvb, wv_scr[...])
+        dcp[rows, :] = mm_nt(dkv_scr[rows, :], wkv_scr[...])
         drt = dk[:, dn:].T
         owner = jnp.where((g == 0) | (g == 3), 0, 1)
         lt0 = (g // 2) * (piece // LANES) + odd * (BLK // LANES)
@@ -445,8 +457,7 @@
     def d_weights(lo_j, hi_j):
         def body(j, cc):
             rows = blk(j)
-            dwk_scr[...] += mm_tn(c_scr[rows, :], dkv_scr[rows, :dn])
-            dwv_scr[...] += mm_tn(c_scr[rows, :], dkv_scr[rows, dn:])
+            dw_scr[...] += mm_tn(c_scr[rows, :], dkv_scr[rows, :])
             return cc
 
         lax.fori_loop(lo_j, hi_j, body, 0)
@@ -459,9 +470,8 @@
                                             send_sem=out_snd.at[w], recv_sem=out_rcv.at[w],
                                             device_id=mate, device_id_type=MESH)
 
-    def x_w(k):
-        s, d = ((dwk_scr, dwk_far), (dwv_scr, dwv_far))[k]
-        return pltpu.make_async_remote_copy(src_ref=s, dst_ref=d, send_sem=out_snd.at[2 + k], recv_sem=out_rcv.at[2 + k],
+    def x_w():
+        return pltpu.make_async_remote_copy(src_ref=dw_scr, dst_ref=dw_far, send_sem=out_snd.at[2], recv_sem=out_rcv.at[2],
                                             device_id=mate, device_id_type=MESH)
 
     def x_q(w):
@@ -474,18 +484,15 @@
         x_o(w).start()
     for g in range(4):
         dqt_scr[g] = jnp.zeros(dqt_scr.shape[1:], F32)
-    dwk_scr[...] = jnp.zeros_like(dwk_scr)
-    dwv_scr[...] = jnp.zeros_like(dwv_scr)
+    dw_scr[...] = jnp.zeros_like(dw_scr)
     lax.fori_loop(0, nb, bwd_block, 0)
 
-    done_a, done_b = len(HOOKS_A), len(HOOKS_B)
-
     def tail(k):
-        run_stage(k, "c")
-        if k + done_b < n_stage:
-            run_stage(k + done_b, "b")
-        if k + done_a < n_stage:
-            run_stage(k + done_a, "a")
+        for core in range(2):
+            items = [(n, k + d) for c, n, d in TAIL if c == core and (k + d > 0) and k + d < n_stage]
+            items += [(n, 0) for c, n, d in TAIL if c == 1 - core and k + d == 0]
+            if items:
+                run_for(core, items)
 
     tail(0)
     for g in range(4):
@@ -496,8 +503,7 @@
     d_weights(0, nb // 2)
     tail(2)
     d_weights(nb // 2, nb)
-    for k in range(2):
-        x_w(k).start()
+    x_w().start()
     tail(3)
     for w in range(2):
         dqt_out[me, :, pl.ds(w * piece, piece)] = dqt_scr[own_piece(w)]
@@ -507,9 +513,9 @@
         mine = o_scr[pl.ds(mul(own_piece(w) * piece, piece), piece), :]
         o_out[pl.ds(w * piece, piece)] = pack(dkv_scr.at[pl.ds(0, piece), :], mine, o_far[pl.ds(w * piece, piece), :])
     tail(5)
-    for k, (s_, f_, o_) in enumerate(((dwk_scr, dwk_far, dwk_out), (dwv_scr, dwv_far, dwv_out))):
-        x_w(k).wait_recv()
-        o_[...] = pack(wide_scr, s_[...], f_[...])
+    x_w().wait_recv()
+    for o_, lo_ in ((dwk_out, 0), (dwv_out, dn)):
+        o_[...] = pack(wide_scr, dw_scr[:, lo_:lo_ + dn], dw_far[:, lo_:lo_ + dn])
     for k in range(6, n_stage):
         tail(k)
     for rt in range(dr // 8):
@@ -520,16 +526,18 @@
     for w in range(2):
         x_q(w).wait()
         x_o(w).wait_send()
-        x_w(w).wait_send()
         for k in range(4):
             in_remote(w, own_piece(w), k).wait_send()
 
-    def drain(un):
-        for cpy in un.all_copies():
-            cpy.wait_send()
-
-    for name in sets:
-        each(name, drain)
+    x_w().wait_send()
+
+    for wh, n in ((0, cols), (1, cols), (2, cols), (3, cols), (4, 2)):
+        def drain(b, cc, wh=wh):
+            un = Unit(wh, b, 0)
+            un.swap().wait_send()
+            return cc
+
+        lax.fori_loop(0, n, drain, 0)
 
 
 def run(c, rt, qt, do, wuk, wuv, side, vmem=51 * 2**20):
@@ -560,14 +568,14 @@
         out_specs=[vm_spec] * 6,
         out_shape=[vm((half, 2, dv), BF), vm((2, qk, half), F32), vm((half + BLK, rank), F32), vm((dr, half), F32),
                    vm((rank, 2, dn), F32), vm((rank, 2, dv), F32)],
-        scratch_shapes=[vm((t, rank), BF), vm((dr, t), BF), vm((qk, t), BF), vm((t, 2, dv), BF), vm((rank, dn), BF), vm((rank, dv), BF),
+        scratch_shapes=[vm((t, rank), BF), vm((dr, t), BF), vm((qk, t), BF), vm((t, 2, dv), BF), vm((rank, dn + dv), BF),
                         vm((t, dv), BF), vm((t, qk), BF), vm((t, dv), BF), vm((4, qk, piece), BF), vm((4, dv, piece), BF),
                         vm((t, dv), BF), vm((1, t), F32), vm((1, t), F32),
                         vm((1, piece), F32), vm((1, piece), F32), vm((dv, piece), F32), vm((4, qk, piece), F32),
                         vm((BLK, qk), F32), vm((BLK, dv), F32), vm((t, dn + dv), BF), vm((rank, 2 * dn), F32),
-                        vm((t + 2 * BLK, rank), F32), vm((rank, dn), F32), vm((rank, dv), F32),
-                        vm((half, dv), BF), vm((rank, dn), F32), vm((rank, dv), F32), vm((nu, BLK, LANES), F32)]
-        + bufs + [dma((4, 2)), dma((4, 2)), dma((4, 2)), dma((nu, 25)), dma((nu, 25)), dma((1,)), dma((8,)), dma((8,))],
+                        vm((t + 2 * BLK, rank), F32), vm((rank, dn + dv), F32),
+                        vm((half, dv), BF), vm((rank, dn + dv), F32), vm((nu, BLK, LANES), F32)]
+        + bufs + [dma((4, 2)), dma((4, 2)), dma((4, 2)), dma((nu, 3)), dma((nu, 25)), dma((6,)), dma((6,))],
         compiler_params=pltpu.CompilerParams(collective_id=0, has_side_effects=True, vmem_limit_bytes=vmem),
         name="mla_step",
     )(c, rt, qt, do, wuk, wuv)

time: 138 us -> 126 us (0.913)
  the two profiles are of different devices: /device:TPU:0 before, /device:TPU:1 now
where the time goes in v5:
time: 126 us
  Pallas kernels  118 us (94%)
  local copies, waits for them, and re-layouts  7.47 us (6%)
    pallas_call x1, Pallas kernels, run(): pl.pallas_call(functools.partial(kernel, side), in_specs=[any_spec] * 4 +...  118 us
    unnamed x5, local copies, waits for them, and re-layouts  5.01 us

profile of v5, /device:TPU:1, one launch (start us, length us, event | category | flops | bytes accessed | tf_op | source)
XLA Modules:
  0.0 126.3 jit_solution(12949871627424744086)
XLA Ops:
  0.6 118.2 %mla_step.1 = (bf16[2048,2,128]{2,1,0:T(2,128)(2,1)S(1)}, f32[2,192,2048]{2,1,0:T(8,128)S(1)}, f32[2560,512]{1,0:T(8,128)S(1)}, f32[64,2048]{1,0:T(8,128)S(1)}, ...) custom-call(bf16[2048,512]{1,0:T(8,128)(2,1)} %c_in.1, bf16[64,2048]{1,0:T(8,128)(2,1)} %bitcast.7, ...), custom_call_target="tpu_custom_call" | custom-call | tf_op jit(solution)/shard_map/mla_step/pallas_call | solution.py:565
  118.8 1.0 copy.17
  119.8 1.7 %copy.18 = f32[2048,2,192]{0,2,1:T(8,128)} copy(f32[2048,2,192]{0,2,1:T(8,128)S(1)} %bitcast.4) | data formatting | bytes 6291456
  121.5 0.8 copy.19
  122.3 0.8 copy.20
  123.1 0.8 copy.21
  123.9 2.5 %slice.3 = f32[2048,512]{1,0:T(8,128)} slice(f32[2560,512]{1,0:T(8,128)S(1)} %get-tuple-element.14), slice={[0:2048], [0:512]} | slice | bytes 8388608 | tf_op jit(solution)/shard_map/slice | solution.py:593

commit v6 on v5

--- a/solution.py
+++ b/solution.py
@@ -11,11 +11,12 @@
 NEG_BIG = -1.0e30
 LOG2E = math.log2(math.e)
 LANES = 128
+WIDE = 256
 BLK = 512
 HOOKS = {2: [(1, "p3", 0)], 5: [(0, "p3", 1)], 8: [(0, "p3", 2)], 10: [(1, "p0", 0)], 11: [(0, "p3", 3)],
          13: [(0, "p3", 4), (0, "p0", 1)], 14: [(0, "p2", 0)], 15: [(0, "p3", 5)], 16: [(0, "p0", 2)],
          17: [(0, "p3", 6), (1, "p2", 1), (0, "p1h", 0)], 19: [(0, "p3", 7), (0, "p0", 3), (1, "p2", 2), (1, "p1h", 1)]}
-TAIL = ((0, "p3", 8), (0, "p0", 4), (1, "p2", 3), (1, "p1h", 2), (1, "p1l", 0))
+TAIL = ((1, "p1l", 0), (0, "p0", 4), (0, "p3", 8), (1, "p1h", 2), (1, "p2", 3))
 MESH = pl.DeviceIdType.MESH
 
 
@@ -37,13 +38,13 @@
            do_scr, kc_scr, v_scr, kt_scr, vt_scr, o_scr, lse_scr, dd_scr,
            m_scr, l_scr, acc_scr, dqt_scr, dk_scr, dv_scr,
            dkv_scr, wide_scr, dcp, dw_scr, o_far, dw_far, d2d,
-           ra1, ra2, rb1, rb2, rc1, rc2,
+           ra1, ra2, far1, far2,
            in_loc, in_snd, in_rcv, x_snd, x_rcv, out_snd, out_rcv):
     tp = lax.axis_index("tp")
     me = lax.axis_index("cp")
     strides = (1, side, side * side)
     coord = [lax.rem(tp // st, side) for st in strides]
-    nbr = [[tp + (lax.rem(coord[a] + off, side) - coord[a]) * strides[a] for off in (1, side - 1)] for a in range(3)]
+    nbr = [[tp + (lax.rem(coord[a] + off, side) - coord[a]) * strides[a] for off in range(1, side)] for a in range(3)]
     mate = {"cp": 1 - me}
     t_all, rank = c_scr.shape
     piece = t_all // 4
@@ -54,17 +55,17 @@
     dr = rt_scr.shape[0]
     scale = qk ** -0.5
     scale2 = scale * LOG2E
-    cols = rank // LANES
+    cols = rank // WIDE
 
     def mul(x, n):
         return pl.multiple_of(x, n)
 
     barrier = pltpu.get_barrier_semaphore()
     for a in range(3):
-        for b in range(2):
+        for b in range(side - 1):
             pl.semaphore_signal(barrier, inc=1, device_id={"tp": nbr[a][b]}, device_id_type=MESH)
     pl.semaphore_signal(barrier, inc=1, device_id=mate, device_id_type=MESH)
-    pl.semaphore_wait(barrier, 7)
+    pl.semaphore_wait(barrier, 3 * (side - 1) + 1)
 
     def own_piece(w):
         return jnp.where(w == 0, me, 3 - me) if not isinstance(w, int) else (me if w == 0 else 3 - me)
@@ -222,26 +223,28 @@
 
     lax.fori_loop(0, 4, fwd_piece, 0)
 
-    rbufs = ((ra1, ra2), (rb1, rb2), (rc1, rc2))
-    sets = {"p3": ((2, cols, 0), (3, cols, 1)), "p0": ((0, cols, 0), (1, cols, 1), (4, 2, 0)),
-            "p2": ((2, cols, 0), (3, cols, 1)), "p1h": ((1, cols, 0),), "p1l": ((0, cols, 0), (4, 2, 1))}
+    sets = {"p3": ((2, cols, 0), (3, cols, 2)), "p0": ((0, cols, 1), (1, cols, 0), (4, 1, 2)),
+            "p2": ((2, cols, 0), (3, cols, 2)), "p1h": ((1, cols, 1),), "p1l": ((0, cols, 0), (4, 1, 2))}
 
     def pick(a, xs):
         return jnp.where(a == 0, xs[0], jnp.where(a == 1, xs[1], xs[2]))
 
+    def wrap(x, n):
+        return jnp.where(x >= n, x - n, x)
+
     class Unit:
         def __init__(self, wh, b, turn):
-            self.wh, self.b = wh, b
+            self.wh = wh
             self.u = wh * cols + b
-            self.lanes = pl.ds(mul(b * LANES, LANES), LANES)
-            first = lax.rem(b + turn, 3)
+            self.lanes = pl.ds(mul(b * WIDE, WIDE), WIDE)
+            first = wrap(b + turn, 3)
             self.level = []
             base, size = 0, BLK
             for t in range(3):
-                a = lax.rem(first + t, 3)
+                a = wrap(first + t, 3)
                 n = size // side
                 here = pick(a, coord)
-                self.level.append((base, n, here, pick(a, [x[0] for x in nbr]), pick(a, [x[1] for x in nbr])))
+                self.level.append((base, n, here, [pick(a, [x[o] for x in nbr]) for o in range(side - 1)]))
                 base, size = base + here * n, n
 
         def part(self, owner, start, n):
@@ -258,109 +261,77 @@
             return sum_out.at[pl.ds(mul(self.wh * BLK + start, 8), n), self.lanes]
 
         def spot(self, t, off, extra=0):
-            base, n, here, _, _ = self.level[t]
-            return base + lax.rem(here + off, side) * n + extra
+            base, n, here, _ = self.level[t]
+            return base + wrap(here + off, side) * n + extra
 
         def copy(self, src, dst, k, dev, slot):
             return pltpu.make_async_remote_copy(src_ref=src, dst_ref=dst, send_sem=x_snd.at[self.u, slot],
                                                 recv_sem=x_rcv.at[self.u, k], device_id=dev, device_id_type=MESH)
 
         def swap(self):
-            return self.copy(self.part(1 - me, 0, BLK), d2d.at[self.u], 0, mate, 2)
-
-        def half(self, t):
-            n = self.level[t][1]
-            return (n // 2, True) if n % 16 == 0 else (n, False)
-
-        def rs(self, t, q):
-            _, n, _, fwd, bwd = self.level[t]
-            h, _ = self.half(t)
-            r1, r2 = rbufs[t]
-            src, dst, dev = ((self.spot(t, 2), r1.at[self.u, 0], fwd), (self.spot(t, 2, h), r1.at[self.u, 1], bwd),
-                             (self.spot(t, 1), r2.at[self.u, 0], fwd), (self.spot(t, side - 1), r2.at[self.u, 1], bwd))[q]
-            return self.copy(self.own(src, h if q < 2 else n), dst, 1 + 4 * t + q, {"tp": dev}, q % 2)
-
-        def ag(self, t, q):
-            _, n, _, fwd, bwd = self.level[t]
-            h, _ = self.half(t)
-            at, m, dev = ((self.spot(t, 0), n, fwd), (self.spot(t, 0), n, bwd),
-                          (self.spot(t, side - 1), h, fwd), (self.spot(t, 1, h), h, bwd))[q]
+            return self.copy(self.part(1 - me, 0, BLK), d2d.at[self.u], 0, mate, 3)
+
+        def near(self, q):
+            _, n, _, dev = self.level[0]
+            h = n // 2
+            src, m, dst, to = ((self.spot(0, 2), h, ra1.at[self.u, 0], 0), (self.spot(0, 2, h), h, ra1.at[self.u, 1], 2),
+                               (self.spot(0, 1), n, ra2.at[self.u, 0], 0), (self.spot(0, side - 1), n, ra2.at[self.u, 1], 2))[q]
+            return self.copy(self.own(src, m), dst, 1 + q, {"tp": dev[to]}, q % 2)
+
+        def back(self, q):
+            _, n, _, dev = self.level[0]
+            h = n // 2
+            at, m, to = ((self.spot(0, 0), n, 0), (self.spot(0, 0), n, 2),
+                         (self.spot(0, side - 1), h, 0), (self.spot(0, 1, h), h, 2))[q]
             r = self.out(at, m)
-            return self.copy(r, r, 13 + 4 * t + q, {"tp": dev}, q % 2)
-
-        def sent(self, k):
-            if k < 1:
-                return []
-            if k < 7:
-                t, second = divmod(k - 1, 2)
-                qs, f = ((2, 3) if second else (0, 1) if self.half(t)[1] else (0,)), self.rs
-            else:
-                t, second = divmod(k - 7, 2)
-                t = 2 - t
-                qs, f = ((0, 1) if not second else (2, 3) if self.half(t)[1] else (2,)), self.ag
-            return [] if t < 0 else [f(t, q) for q in qs]
-
-        def start_rs(self, t):
-            self.rs(t, 0).start()
-            if self.half(t)[1]:
-                self.rs(t, 1).start()
-
-        def start_ag(self, t):
-            self.ag(t, 0).start()
-            self.ag(t, 1).start()
+            return self.copy(r, r, 5 + q, {"tp": dev[to]}, q % 2)
+
+        def direct(self, t, o):
+            _, n, _, dev = self.level[t]
+            return self.copy(self.own(self.spot(t, o + 1), n), (far1, far2)[t - 1].at[self.u, o], 9 + 3 * (t - 1) + o,
+                             {"tp": dev[o]}, o)
+
+        def share(self, t, o):
+            _, n, _, dev = self.level[t]
+            r = self.out(self.spot(t, 0), n)
+            return self.copy(r, r, 15 + 3 * (t - 1) + o, {"tp": dev[o]}, o)
+
+        def started(self, k):
+            return {1: lambda: [self.near(0), self.near(1)], 2: lambda: [self.near(2), self.near(3)],
+                    3: lambda: [self.direct(1, o) for o in range(3)], 4: lambda: [self.direct(2, o) for o in range(3)],
+                    5: lambda: [self.share(2, o) for o in range(3)], 6: lambda: [self.share(1, o) for o in range(3)],
+                    7: lambda: [self.back(0), self.back(1)], 8: lambda: [self.back(2), self.back(3)]}.get(k, lambda: [])()
 
         def stage(self, k):
-            for cpy in self.sent(k - 1):
+            for cpy in self.started(k - 1):
                 cpy.wait_send()
+            u = self.u
             if k == 1:
                 self.swap().wait_recv()
                 r = self.own(0, BLK)
-                r[...] = r[...] + d2d[self.u]
-                self.start_rs(0)
-            elif k < 8:
-                t, last = divmod(k - 2, 2)
-                n = self.level[t][1]
-                h, two = self.half(t)
-                r1, r2 = rbufs[t]
-                if not last:
-                    self.rs(t, 0).wait_recv()
-                    p = self.own(self.spot(t, 1), h)
-                    p[...] = p[...] + r1[self.u, 0]
-                    self.rs(t, 2).start()
-                    if two:
-                        self.rs(t, 1).wait_recv()
-                        p = self.own(self.spot(t, side - 1, h), h)
-                        p[...] = p[...] + r1[self.u, 1]
-                    self.rs(t, 3).start()
-                else:
-                    self.rs(t, 2).wait_recv()
-                    self.rs(t, 3).wait_recv()
-                    p = self.own(self.spot(t, 0), n)
-                    total = p[...] + r2[self.u, 0] + r2[self.u, 1]
-                    if t < 2:
-                        p[...] = total
-                        self.start_rs(t + 1)
-                    else:
-                        self.out(self.spot(t, 0), n)[...] = total
-                        self.start_ag(2)
-            else:
-                t, last = divmod(k - 8, 2)
-                t = 2 - t
-                two = self.half(t)[1]
-                if not last:
-                    self.ag(t, 0).wait_recv()
-                    self.ag(t, 2).start()
-                    self.ag(t, 1).wait_recv()
-                    if two:
-                        self.ag(t, 3).start()
-                else:
-                    self.ag(t, 2).wait_recv()
-                    if two:
-                        self.ag(t, 3).wait_recv()
-                    if t > 0:
-                        self.start_ag(t - 1)
-
-    n_stage = 14
+                r[...] = r[...] + d2d[u]
+            elif k == 2:
+                h = self.level[0][1] // 2
+                for q, at in ((0, self.spot(0, 1)), (1, self.spot(0, side - 1, h))):
+                    self.near(q).wait_recv()
+                    p = self.own(at, h)
+                    p[...] = p[...] + ra1[u, q]
+            elif k in (3, 4, 5):
+                t = k - 3
+                for cpy in ([self.near(2), self.near(3)] if t == 0 else [self.direct(t, o) for o in range(3)]):
+                    cpy.wait_recv()
+                at, n = self.spot(t, 0), self.level[t][1]
+                total = self.own(at, n)[...]
+                for o in range(2 if t == 0 else 3):
+                    total = total + (ra2, far1, far2)[t][u, o]
+                (self.out if t == 2 else self.own)(at, n)[...] = total
+            elif k > 5:
+                for cpy in self.started(k - 1):
+                    cpy.wait_recv()
+            for cpy in self.started(k):
+                cpy.start()
+
+    n_stage = 10
 
     def each(name, fn):
         for wh, n, turn in sets[name]:
@@ -531,7 +502,7 @@
 
     x_w().wait_send()
 
-    for wh, n in ((0, cols), (1, cols), (2, cols), (3, cols), (4, 2)):
+    for wh, n in ((0, cols), (1, cols), (2, cols), (3, cols), (4, 1)):
         def drain(b, cc, wh=wh):
             un = Unit(wh, b, 0)
             un.swap().wait_send()
@@ -549,7 +520,7 @@
     dv = wuv.shape[2]
     nb = t // BLK
     piece = t // 4
-    nu = 4 * (rank // LANES) + 2
+    nu = 4 * (rank // WIDE) + 1
     sds = jax.ShapeDtypeStruct
     vm = pltpu.VMEM
     bufs = []
@@ -557,7 +528,8 @@
     for _ in range(3):
         n = size // side
         h = n // 2 if n % 16 == 0 else n
-        bufs += [vm((nu, 2, h, LANES), F32), vm((nu, 2, n, LANES), F32)]
+        bufs += [vm((nu, 2, h, WIDE), F32)] if not bufs else []
+        bufs += [vm((nu, 2 if size == BLK else 3, n, WIDE), F32)]
         size = n
     dma = pltpu.SemaphoreType.DMA
     any_spec = pl.BlockSpec(memory_space=pl.ANY)
@@ -574,11 +546,39 @@
                         vm((1, piece), F32), vm((1, piece), F32), vm((dv, piece), F32), vm((4, qk, piece), F32),
                         vm((BLK, qk), F32), vm((BLK, dv), F32), vm((t, dn + dv), BF), vm((rank, 2 * dn), F32),
                         vm((t + 2 * BLK, rank), F32), vm((rank, dn + dv), F32),
-                        vm((half, dv), BF), vm((rank, dn + dv), F32), vm((nu, BLK, LANES), F32)]
-        + bufs + [dma((4, 2)), dma((4, 2)), dma((4, 2)), dma((nu, 3)), dma((nu, 25)), dma((6,)), dma((6,))],
+                        vm((half, dv), BF), vm((rank, dn + dv), F32), vm((nu, BLK, WIDE), F32)]
+        + bufs + [dma((4, 2)), dma((4, 2)), dma((4, 2)), dma((nu, 4)), dma((nu, 21)), dma((6,)), dma((6,))],
         compiler_params=pltpu.CompilerParams(collective_id=0, has_side_effects=True, vmem_limit_bytes=vmem),
         name="mla_step",
     )(c, rt, qt, do, wuk, wuv)
+
+
+def store_kernel(*refs):
+    n = (len(refs) - 1) // 2
+    sem = refs[-1]
+    copies = []
+    for k in range(n):
+        src, dst = refs[k], refs[n + k]
+        if src.shape != dst.shape:
+            src = src.at[pl.ds(0, dst.shape[0]), :]
+        copies.append(pltpu.make_async_copy(src, dst, sem.at[k]))
+    for cpy in copies:
+        cpy.start()
+    for cpy in copies:
+        cpy.wait()
+
+
+def store_all(arrays, shapes):
+    n = len(arrays)
+    return pl.pallas_call(
+        store_kernel,
+        in_specs=[pl.BlockSpec(memory_space=pltpu.VMEM)] * n,
+        out_specs=[pl.BlockSpec(memory_space=pl.ANY)] * n,
+        out_shape=[pltpu.HBM(sh, a.dtype) for a, sh in zip(arrays, shapes)],
+        scratch_shapes=[pltpu.SemaphoreType.DMA((n,))],
+        compiler_params=pltpu.CompilerParams(vmem_limit_bytes=2**20),
+        name="store_all",
+    )(*arrays)
 
 
 def solution(mesh):
@@ -589,8 +589,10 @@
     grad_spec = P('dp', 'tp', None)
 
     def device_fn(c_latent, k_rope, q_heads, d_out, w_uk, w_uv):
-        o, dqt, dc, drt, dwk, dwv = run(c_latent, k_rope.T, jnp.transpose(q_heads, (1, 2, 0)), d_out, w_uk, w_uv, side)
-        return o, jnp.transpose(dqt, (2, 0, 1)), dc[:c_latent.shape[0]], drt.T, dwk, dwv
+        outs = run(c_latent, k_rope.T, jnp.transpose(q_heads, (1, 2, 0)), d_out, w_uk, w_uv, side)
+        shapes = [c_latent.shape if k == 2 else x.shape for k, x in enumerate(outs)]
+        o, dqt, dc, drt, dwk, dwv = store_all(outs, shapes)
+        return o, jnp.transpose(dqt, (2, 0, 1)), dc, drt.T, dwk, dwv
 
     return jax.shard_map(device_fn, mesh=mesh,
                          in_specs=(seq_spec, seq_spec, head_spec, head_spec, weight_spec, weight_spec),

time: 126 us -> 118 us (0.937)
  local copies, waits for them, and re-layouts: 7.47 us -> 0 us
    pallas_call x1, Pallas kernels: 118 us -> 113 us  [run(): pl.pallas_call(functools.partial(kernel, side), in_specs=[any_spec] * 4 +...]
    unnamed x5 -> x0, local copies, waits for them, and re-layouts: 5.01 us -> none
    pallas_call x0 -> x1, Pallas kernels: none -> 3.81 us  [store_all(): pl.pallas_call(store_kernel, in_specs=[pl.BlockSpec(memory_space=pltpu.VM...]
    slice x1 -> x0, local copies, waits for them, and re-layouts: 2.45 us -> none  [device_fn(): dc[:c_latent.shape[0]]]
where the time goes in v6:
time: 118 us; the launch traced here: 117 us
  Pallas kernels  117 us (99%)
    pallas_call x1, Pallas kernels, run(): pl.pallas_call(functools.partial(kernel, side), in_specs=[any_spec] * 4 +...  113 us
    pallas_call x1, Pallas kernels, store_all(): pl.pallas_call(store_kernel, in_specs=[pl.BlockSpec(memory_space=pltpu.VM...  3.81 us

profile of v6, /device:TPU:1, one launch (start us, length us, event | category | flops | bytes accessed | tf_op | source)
XLA Modules:
  0.0 117.4 jit_solution(3323931404924475165)
XLA Ops:
  0.6 112.8 %mla_step.1 = (bf16[2048,2,128]{2,1,0:T(2,128)(2,1)S(1)}, f32[2,192,2048]{2,1,0:T(8,128)S(1)}, f32[2560,512]{1,0:T(8,128)S(1)}, f32[64,2048]{1,0:T(8,128)S(1)}, ...) custom-call(bf16[2048,512]{1,0:T(8,128)(2,1)} %c_in.1, bf16[64,2048]{1,0:T(8,128)(2,1)} %bitcast.5, ...), custom_call_target="tpu_custom_call" | custom-call | tf_op jit(solution)/shard_map/mla_step/pallas_call | solution.py:537
  113.5 3.8 %store_all.1 = (bf16[2048,2,128]{2,1,0:T(2,128)(2,1)}, f32[2,192,2048]{2,1,0:T(8,128)}, f32[2048,512]{1,0:T(8,128)}, f32[64,2048]{1,0:T(8,128)}, f32[512,2,128]{2,1,0:T(2,128)}, /*index=5*/f32[512,2,128]{2,1,0:T(2,128)}) custom-call(bf16[2048,2,128]{2,1,0:T(2,128)(2,1)S(1)} %get-tuple-element.18.refs_0_, f32[2,192,2048]{2,1,0:T(8,128)S(1)} %get-tuple-element.19.refs_1_, ...), custom_call_target="tpu_custom_call" | custom-call | tf_op jit(solution)/shard_map/store_all/pallas_call | solution.py:573

commit v7 on v6

--- a/solution.py
+++ b/solution.py
@@ -13,10 +13,12 @@
 LANES = 128
 WIDE = 256
 BLK = 512
-HOOKS = {2: [(1, "p3", 0)], 5: [(0, "p3", 1)], 8: [(0, "p3", 2)], 10: [(1, "p0", 0)], 11: [(0, "p3", 3)],
-         13: [(0, "p3", 4), (0, "p0", 1)], 14: [(0, "p2", 0)], 15: [(0, "p3", 5)], 16: [(0, "p0", 2)],
-         17: [(0, "p3", 6), (1, "p2", 1), (0, "p1h", 0)], 19: [(0, "p3", 7), (0, "p0", 3), (1, "p2", 2), (1, "p1h", 1)]}
-TAIL = ((1, "p1l", 0), (0, "p0", 4), (0, "p3", 8), (1, "p1h", 2), (1, "p2", 3))
+ORDER = (7, 6, 1, 5, 4, 0, 3, 2)
+SLOTS = (0, 1, 2, 6, 8, 10, 14, 17)
+HOOKS = {2: [(1, "p3", 0)], 5: [(0, "p3", 1)], 8: [(0, "p3", 2)], 10: [(0, "p2", 0)], 11: [(0, "p3", 3)],
+         13: [(0, "p3", 4), (1, "p2", 1)], 14: [(1, "p0", 0)], 15: [(0, "p3", 5), (1, "p2", 2)], 16: [(0, "p0", 1)],
+         17: [(0, "p3", 6), (0, "p1h", 0), (1, "p2", 3)], 19: [(0, "p3", 7), (0, "p0", 2), (1, "p1h", 1)]}
+TAIL = ((1, "p1l", 0), (0, "p0", 3), (0, "p3", 8), (1, "p1h", 2), (1, "p2", 4))
 MESH = pl.DeviceIdType.MESH
 
 
@@ -381,11 +383,13 @@
             dv_scr[...] += dv_blk
 
     def bwd_block(step, carry):
-        pair, low = step // per, lax.rem(step, per)
-        g = jnp.where(pair == 0, 3, jnp.where(pair == 1, 0, jnp.where(pair == 2, 2, 1)))
-        j = g * per + 1 - low
-        odd = 1 - low
-        t0 = jnp.where(pair == 0, low, jnp.where(pair == 1, 2 + 4 * low, jnp.where(pair == 2, 10 + 2 * low, 14 + 3 * low)))
+        j, t0 = ORDER[0], SLOTS[0]
+        for k in range(1, len(ORDER)):
+            past = (step + nb - k) // nb
+            j = j + (ORDER[k] - ORDER[k - 1]) * past
+            t0 = t0 + (SLOTS[k] - SLOTS[k - 1]) * past
+        g = j // per
+        odd = lax.rem(j, per)
         off = mul(odd * BLK, BLK)
 
         def body(i, cc):
@@ -468,13 +472,13 @@
     tail(0)
     for g in range(4):
         dqt_scr[g] = dqt_scr[g] * scale
-    for w in range(2):
-        x_q(w).start()
     tail(1)
     d_weights(0, nb // 2)
     tail(2)
     d_weights(nb // 2, nb)
     x_w().start()
+    for w in range(2):
+        x_q(w).start()
     tail(3)
     for w in range(2):
         dqt_out[me, :, pl.ds(w * piece, piece)] = dqt_scr[own_piece(w)]

time: 118 us -> 119 us (level)
  no operation moved by 1% of the time
where the time goes in v7:
time: 119 us; the launch traced here: 118 us
  Pallas kernels  118 us (99%)
    pallas_call x1, Pallas kernels, run(): pl.pallas_call(functools.partial(kernel, side), in_specs=[any_spec] * 4 +...  114 us
    pallas_call x1, Pallas kernels, store_all(): pl.pallas_call(store_kernel, in_specs=[pl.BlockSpec(memory_space=pltpu.VM...  3.81 us

profile of v7, /device:TPU:1, one launch (start us, length us, event | category | flops | bytes accessed | tf_op | source)
XLA Modules:
  0.0 118.4 jit_solution(16299504591393603241)
XLA Ops:
  0.6 113.8 %mla_step.1 = (bf16[2048,2,128]{2,1,0:T(2,128)(2,1)S(1)}, f32[2,192,2048]{2,1,0:T(8,128)S(1)}, f32[2560,512]{1,0:T(8,128)S(1)}, f32[64,2048]{1,0:T(8,128)S(1)}, ...) custom-call(bf16[2048,512]{1,0:T(8,128)(2,1)} %c_in.1, bf16[64,2048]{1,0:T(8,128)(2,1)} %bitcast.5, ...), custom_call_target="tpu_custom_call" | custom-call | tf_op jit(solution)/shard_map/mla_step/pallas_call | solution.py:541
  114.4 3.8 %store_all.1 = (bf16[2048,2,128]{2,1,0:T(2,128)(2,1)}, f32[2,192,2048]{2,1,0:T(8,128)}, f32[2048,512]{1,0:T(8,128)}, f32[64,2048]{1,0:T(8,128)}, f32[512,2,128]{2,1,0:T(2,128)}, /*index=5*/f32[512,2,128]{2,1,0:T(2,128)}) custom-call(bf16[2048,2,128]{2,1,0:T(2,128)(2,1)S(1)} %get-tuple-element.18.refs_0_, f32[2,192,2048]{2,1,0:T(8,128)S(1)} %get-tuple-element.19.refs_1_, ...), custom_call_target="tpu_custom_call" | custom-call | tf_op jit(solution)/shard_map/store_all/pallas_call | solution.py:577
